TPU v7x, 512 devices: a 4x2x32 block of a 4x16x32 slice. The times are simulated.
512 devices in a mesh: groups: 2 (over y), row: 32 (over z), col: 4 (over x), chan: 2 (over core).
Axes of the slice: x: 4, y: 2, z: 32, core: 2. Of those that a mesh axis runs over, the one named last changes fastest.
The devices are a block of a 4x16x32 slice.
Arguments:
- pair_rep: bfloat16 [512, 256, 128], P(('groups', 'row'), 'col'), parts along dimension 0, may hold values from -6 to 6
- pair_mask: int32 [512, 256], P(('groups', 'row'), 'col'), parts along dimension 0, may hold values 0 or 1
- w_qkvg: bfloat16 [4, 128, 128], P(None, None, 'chan'), may hold values from -0.5 to 0.5
- w_bias: bfloat16 [128, 4], P(None, 'chan'), may hold values from -11 to 11
- w_out: bfloat16 [128, 128], P('chan'), may hold values from -0.5 to 0.5
- cotangent: bfloat16 [512, 256, 128], P(('groups', 'row'), 'col'), parts along dimension 0, may hold values from -6 to 6
Outputs:
- pair_update: bfloat16 [512, 256, 128], P(('groups', 'row'), 'col'), parts along dimension 0
- pair_grad: bfloat16 [512, 256, 128], P(('groups', 'row'), 'col'), parts along dimension 0
- qkvg_grad: float32 [8, 128, 128], P('groups', None, 'chan'), parts along dimension 0
- bias_weight_grad: float32 [256, 4], P('groups', 'chan'), parts along dimension 0
- out_weight_grad: float32 [128, 256], P('chan', 'groups'), parts along dimension 1
There are 2 independent parts, one for each index of `groups`. A program takes and returns all parts, laid end to end along the dimension named above; an argument that names none is the same for every part. Nothing has to cross between parts.
All inputs are finite; a program needn't handle non-finite values. No bound on the sum of `pair_mask` on one device may be relied on, other than what follows from the above.
Results may differ from a plain program's by a relative error of at most 0.035.
The roundings to bfloat16 on the way count: a program that leaves them out, or rounds other values in their place, can miss the bound.
Values may be sent and summed in bfloat16 or wider, within the bound.
A program may use at most 64 MiB of HBM per device.

v0:
```python
import functools

import jax
import jax.numpy as jnp
from jax import lax
from jax.sharding import PartitionSpec as P

EPSILON = 1e-05
MASK_BIG = 1000000000.0


def gathered_by_axis(value, axes, dim):
    for axis in reversed(axes):
        value = lax.all_gather(value, axis, axis=dim, tiled=True)
    return value


def cut_along(value, dim, length):
    before, after = (value.shape[:dim], value.shape[dim + 1 :])
    return jnp.moveaxis(value.reshape(*before, length, -1, *after), dim, 0)


def sent_and_summed(value, axis, dim):
    length = lax.axis_size(axis)
    pieces = lax.all_to_all(cut_along(value, dim, length), axis, 0, 0, tiled=True)
    return jnp.sum(pieces.astype(jnp.float32), axis=0)


def sent_together(arrays, axis, dim, along):
    columns = [a.reshape(*a.shape[:along], -1) for a in arrays]
    both = jnp.concatenate(columns, axis=along)
    result, at, gathered = (lax.all_gather(both, axis, axis=dim, tiled=True), 0, [])
    for a, column in zip(arrays, columns):
        piece = result[..., at : at + column.shape[along]]
        gathered.append(piece.reshape(*piece.shape[:along], *a.shape[along:]))
        at += column.shape[along]
    return tuple(gathered)


def one_axis_at_a_time(value, axes):
    return functools.reduce(lax.psum, axes, value)


def copy_for_each(value, axis):
    copies = jnp.broadcast_to(value, (lax.axis_size(axis), *value.shape))
    return lax.all_to_all(copies, axis, split_axis=0, concat_axis=0, tiled=True)


def of_everyone(value, axis):
    everything = copy_for_each(value, axis)
    return jnp.sum(everything.astype(jnp.float32), axis=0)


def standardize(pair_rep):
    values = pair_rep.astype(jnp.float32)
    centred = values - jnp.mean(values, -1, keepdims=True)
    inv_scale = lax.rsqrt(jnp.mean(centred * centred, -1, keepdims=True) + EPSILON)
    return (centred * inv_scale, inv_scale)


def bias_rows_from(bias_tile):
    head_count, row_count, col_count = bias_tile.shape
    row_devices = lax.axis_size("row")
    col_devices = lax.axis_size("col")
    row_ratio = row_devices // col_devices
    gathered = gathered_by_axis(bias_tile[None], ("row", "col"), 0)
    grouped = gathered.reshape(
        col_devices, row_ratio, col_devices, head_count, row_count, col_count
    )
    own_block = lax.dynamic_index_in_dim(grouped, lax.axis_index("col"), 0, keepdims=False)
    arranged = own_block.transpose(2, 0, 3, 1, 4)
    return arranged.reshape(head_count, row_ratio * row_count, col_devices * col_count)


def bias_tile_from(bias_rows, row_count):
    head_count, col_count, token_count = bias_rows.shape
    row_devices = lax.axis_size("row")
    col_devices = lax.axis_size("col")
    row_ratio = row_devices // col_devices
    tile_cols = token_count // col_devices
    pieces = bias_rows.reshape(head_count, row_ratio, row_count, col_devices, tile_cols)
    pieces = pieces.transpose(3, 1, 0, 2, 4).reshape(row_devices, head_count, row_count, tile_cols)
    summed_tile = sent_and_summed(pieces.astype(jnp.bfloat16), "row", 0)[0]
    gathered = gathered_by_axis(summed_tile[None], ("row", "col"), 0)
    row_index = lax.axis_index("row")
    source = (
        lax.axis_index("col") * row_ratio + row_index % row_ratio
    ) * col_devices + row_index // row_ratio
    result = lax.dynamic_index_in_dim(gathered, source, 0, keepdims=False)
    return result


def on_device(pair_rep, pair_mask, w_qkvg, w_bias, w_out, cotangent):
    full_rows, col_count, channels = pair_rep.shape
    standard_full, inv_full = standardize(pair_rep)
    normed_full = standard_full.astype(jnp.bfloat16)
    local_width = w_qkvg.shape[2]
    head_count = w_bias.shape[1]
    head_size = local_width // head_count
    query_scale = head_size ** (-0.5)
    projected = jnp.einsum("ijc,pce->pije", normed_full, w_qkvg, preferred_element_type=jnp.float32)
    query = (projected[0] * query_scale).astype(jnp.bfloat16)
    key_value = jnp.concatenate([projected[1], projected[2]], -1).astype(jnp.bfloat16)
    gate_act = jax.nn.sigmoid(projected[3])
    bias_tile = jnp.einsum("ijc,ch->hij", normed_full, w_bias, preferred_element_type=jnp.float32)
    bias_rows = bias_rows_from(bias_tile)
    mask_vals = pair_mask.astype(jnp.bfloat16)
    key_values, mask_rows = sent_together((key_value, mask_vals), "col", 1, 2)
    token_count = key_values.shape[1]
    stride = 4
    shaped = (stride, col_count, head_count, head_size)
    long_shape = (stride, token_count, head_count, head_size)

    def split(values):
        return values.reshape((full_rows // stride, stride) + values.shape[1:])

    def attend(running, inputs):
        query_block, kv_block, mask_block, gate_block, cot_block = inputs
        queries = query_block.reshape(shaped)
        keys = kv_block[..., :local_width].reshape(long_shape)
        values_b = kv_block[..., local_width:].reshape(long_shape)
        scores = jnp.einsum("bjhd,bkhd->bhjk", queries, keys, preferred_element_type=jnp.float32)
        scores = (
            scores
            + bias_rows[None]
            + MASK_BIG * (mask_block.astype(jnp.float32)[:, None, None, :] - 1.0)
        )
        weights = jax.nn.softmax(scores, axis=-1)
        weights_b = weights.astype(jnp.bfloat16)
        attended = jnp.einsum(
            "bhjk,bkhd->bjhd", weights_b, values_b, preferred_element_type=jnp.float32
        )
        gate_shaped = gate_block.reshape(shaped)
        gated = (
            (gate_shaped * attended).astype(jnp.bfloat16).reshape(stride, col_count, local_width)
        )
        partial_update = jnp.einsum("bje,ec->bjc", gated, w_out, preferred_element_type=jnp.float32)
        d_gated = jnp.einsum(
            "bjc,ec->bje", cot_block, w_out, preferred_element_type=jnp.float32
        ).reshape(shaped)
        d_gate = d_gated * attended * gate_shaped * (1.0 - gate_shaped)
        d_attended = (d_gated * gate_shaped).astype(jnp.bfloat16)
        d_weights = jnp.einsum(
            "bjhd,bkhd->bhjk", d_attended, values_b, preferred_element_type=jnp.float32
        )
        row_dot = jnp.sum(d_attended.astype(jnp.float32) * attended, -1).transpose(0, 2, 1)[
            ..., None
        ]
        d_scores = weights * (d_weights - row_dot)
        d_scores_b = d_scores.astype(jnp.bfloat16)
        d_query = (
            jnp.einsum("bhjk,bkhd->bjhd", d_scores_b, keys, preferred_element_type=jnp.float32)
            * query_scale
        )
        d_key = jnp.einsum(
            "bhjk,bjhd->bkhd", d_scores_b, queries, preferred_element_type=jnp.float32
        )
        d_value = jnp.einsum(
            "bhjk,bjhd->bkhd", weights_b, d_attended, preferred_element_type=jnp.float32
        )
        d_keyval = jnp.concatenate(
            [
                d_key.reshape(stride, token_count, local_width),
                d_value.reshape(stride, token_count, local_width),
            ],
            -1,
        )
        running = running + jnp.sum(d_scores, 0)
        return (
            running,
            (
                partial_update,
                d_query.reshape(stride, col_count, local_width),
                d_gate.reshape(stride, col_count, local_width),
                d_keyval,
                gated,
            ),
        )

    start = jnp.zeros((head_count, col_count, token_count), jnp.float32)
    inputs = (split(query), split(key_values), split(mask_rows), split(gate_act), split(cotangent))
    bias_sum, stacked = lax.scan(attend, start, inputs)
    update_part = stacked[0].reshape(full_rows, col_count, channels)
    d_query_all = stacked[1].reshape(full_rows, col_count, local_width)
    d_gate_all = stacked[2].reshape(full_rows, col_count, local_width)
    d_keyval_all = stacked[3].reshape(full_rows, token_count, 2 * local_width)
    gated_all = stacked[4].reshape(full_rows, col_count, local_width)
    key_grads = sent_and_summed(d_keyval_all.astype(jnp.bfloat16), "col", 1)
    d_proj = jnp.stack(
        [d_query_all, key_grads[..., :local_width], key_grads[..., local_width:], d_gate_all]
    ).astype(jnp.bfloat16)
    bias_grad_tile = bias_tile_from(bias_sum, full_rows)
    d_normed = jnp.einsum("pije,pce->ijc", d_proj, w_qkvg, preferred_element_type=jnp.float32)
    d_normed = d_normed + jnp.einsum(
        "hij,ch->ijc", bias_grad_tile, w_bias.astype(jnp.float32), precision=lax.Precision.HIGHEST
    )
    qkvg_part = (
        jnp.einsum("ijc,pije->pce", normed_full, d_proj, preferred_element_type=jnp.float32)
        / token_count
    )
    bias_part = (
        jnp.einsum(
            "ijc,hij->ch",
            normed_full.astype(jnp.float32),
            bias_grad_tile,
            precision=lax.Precision.HIGHEST,
        )
        / token_count
    )
    out_part = (
        jnp.einsum("ije,ijc->ec", gated_all, cotangent, preferred_element_type=jnp.float32)
        / token_count
    )
    qkvg_grad, bias_weight_grad, out_weight_grad = (
        one_axis_at_a_time(qkvg_part, ("row", "col")),
        one_axis_at_a_time(bias_part, ("row", "col")),
        one_axis_at_a_time(out_part, ("row", "col")),
    )
    update_sum, d_total = (
        of_everyone(update_part.astype(jnp.bfloat16), "chan").astype(jnp.float32),
        of_everyone(d_normed.astype(jnp.bfloat16), "chan").astype(jnp.float32),
    )
    centred_grad = d_total - jnp.mean(d_total, -1, keepdims=True)
    centred_grad = centred_grad - standard_full * jnp.mean(
        d_total * standard_full, -1, keepdims=True
    )
    update_out = update_sum.astype(jnp.bfloat16)
    pair_grad = (inv_full * centred_grad).astype(jnp.bfloat16)
    return (update_out, pair_grad, qkvg_grad, bias_weight_grad, out_weight_grad)


def solution(mesh):
    in_specs = (
        P(("groups", "row"), "col", None),
        P(("groups", "row"), "col"),
        P(None, None, "chan"),
        P(None, "chan"),
        P("chan", None),
        P(("groups", "row"), "col", None),
    )
    out_specs = (
        P(("groups", "row"), "col", None),
        P(("groups", "row"), "col", None),
        P("groups", None, "chan"),
        P("groups", "chan"),
        P("chan", "groups"),
    )
    return jax.shard_map(
        on_device, mesh=mesh, in_specs=in_specs, out_specs=out_specs, check_vma=False
    )
```

profile of v0, /device:TPU:40, one launch (start us, length us, event | category | flops | bytes accessed | tf_op | source)
XLA Modules:
  0.0 515.5 jit_solution(4080909957557177124)
XLA Ops:
  7.3 0.7 convert_bitcast_fusion
  8.0 1.0 convert_reduce_fusion.2
  9.1 0.3 fusion.29
  9.5 0.4 fusion.53
  10.1 15.4 %all_gather.15 = bf16[8,256,129]{2,1,0:T(8,128)(2,1)S(1)} all-gather(bf16[8,64,129]{2,1,0:T(8,128)(2,1)S(1)} %pad_maximum_fusion.1), channel_id=1, replica_groups=mesh['groups'=2,'row'=32,'col'=4,'chan'=2] {'col'}, dimensions={1}, use_global_device_ids=true | all-gather | bytes 660480 | tf_op jit(solution)/shard_map/all_gather | solution.py:32
  25.5 0.2 slice_reduce_fusion
  25.7 0.8 copy-done.1
  26.4 0.7 copy-done.15
  27.1 0.3 convolution_bitcast_fusion.6
  27.4 12.2 %all-gather = f32[8,8,64]{2,1,0:T(8,128)S(1)} all-gather(f32[2,8,64]{2,1,0:T(8,128)S(1)} %copy.85), channel_id=2, replica_groups=mesh['groups'=2,'row'=32,'col'=4,'chan'=2] {'col'}, dimensions={0}, use_global_device_ids=true | all-gather | bytes 20480 | tf_op jit(solution)/shard_map/all_gather | solution.py:14
  39.6 100.6 %all_gather.17 = f32[128,2,8,64]{3,2,1,0:T(8,128)S(1)} all-gather(f32[4,2,8,64]{3,2,1,0:T(8,128)S(1)} %bitcast.266), channel_id=1, replica_groups=mesh['groups'=2,'row'=32,'col'=4,'chan'=2] {'row'}, dimensions={0}, use_global_device_ids=true | all-gather | bytes 540672 | tf_op jit(solution)/shard_map/all_gather | solution.py:14
  140.4 0.2 add.154
  140.7 0.4 copy-done.5
  141.1 0.5 slice-done
  141.6 0.2 copy-done.3
  141.8 11.5 %while.24 = (s32[]{:T(128)}, f32[2,64,256]{2,1,0:T(8,128)S(1)}, bf16[2,4,64,128]{3,2,1,0:T(8,128)(2,1)S(1)}, bf16[2,4,64,64]{2,3,1,0:T(8,128)(2,1)}, bf16[2,4,64...) while((s32[]{:T(128)}, f32[2,64,256]{2,1,0:T(8,128)S(1)}, ...), condition=%wide.wide.region_7.8_spmd.clone, body=%wide.wide.region_2.7_spmd.clone.sunk | while | flops 60951296 | bytes 14766459 | solution.py:182
  141.9 0.2 fusion.135
  142.5 0.5 fusion.137
  143.1 0.2 multiply_reduce_fusion.3
  143.5 0.3 fusion.139
  143.9 0.2 convolution_multiply_fusion.3
  144.1 0.6 constant_dynamic-update-slice_fusion.10
  145.1 0.2 fusion.140
  145.4 0.5 copy-done.12
  145.8 0.2 copy-done.9
  146.2 0.6 copy-done.10
  146.8 0.8 copy-done.7
  148.2 0.5 fusion.137
  148.8 0.2 multiply_reduce_fusion.3
  149.3 0.3 fusion.139
  149.6 0.2 convolution_multiply_fusion.3
  149.9 0.6 constant_dynamic-update-slice_fusion.10
  150.9 0.2 fusion.140
  151.1 0.5 copy-done.12
  151.6 0.2 copy-done.9
  151.9 0.6 copy-done.10
  152.5 0.8 copy-done.7
  153.3 0.8 broadcast_in_dim.68
  154.1 3.5 all-to-all-start
  157.6 0.8 copy.92
  158.4 0.7 all-to-all-done
  159.1 4.3 all-to-all-start.1
  163.6 0.8 reshape.180
  164.3 1.1 copy.90
  165.5 0.7 reduce_sum.115
  166.2 0.2 copy-done.11
  166.4 0.2 fusion.18
  166.6 6.5 %all-to-all-done.1 = bf16[4,8,64,128]{3,2,1,0:T(8,128)(2,1)S(1)} async-done(((bf16[4,8,64,128]{3,2,1,0:T(8,128)(2,1)}), bf16[4,8,64,128]{3,2,1,0:T(8,128)(2,1)S(1)}, u32[]{:S(2)}, u32[]{:S(2)}) %all-to-all-start.1) | async-done | bytes 524320 | tf_op jit(solution)/shard_map/all_to_all | solution.py:25
  173.2 5.3 %all-to-all-start.2 = ((bf16[32,2,512]{2,1,0:T(2,128)(2,1)}), bf16[32,2,512]{2,1,0:T(2,128)(2,1)S(1)}, u32[]{:S(2)}, u32[]{:S(2)}) async-start(bf16[32,2,512]{2,1,0:T(2,128)(2,1)} %reshape.180), calls=%async_computation.2 | async-start | bytes 131072 | tf_op jit(solution)/shard_map/all_to_all | solution.py:25
  178.7 1.1 fusion.17
  180.0 0.3 convolution_bitcast_fusion.3
  180.3 22.6 %all-to-all-done.2 = bf16[32,2,512]{2,1,0:T(2,128)(2,1)S(1)} async-done(((bf16[32,2,512]{2,1,0:T(2,128)(2,1)}), bf16[32,2,512]{2,1,0:T(2,128)(2,1)S(1)}, u32[]{:S(2)}, u32[]{:S(2)}) %all-to-all-start.2) | async-done | bytes 65568 | tf_op jit(solution)/shard_map/all_to_all | solution.py:25
  203.1 12.0 %all-gather.1 = f32[8,8,64]{2,1,0:T(8,128)S(1)} all-gather(f32[2,8,64]{2,1,0:T(8,128)S(1)} %convert_reduce_fusion.3), channel_id=3, replica_groups=mesh['groups'=2,'row'=32,'col'=4,'chan'=2] {'col'}, dimensions={0}, use_global_device_ids=true | all-gather | bytes 20480 | tf_op jit(solution)/shard_map/all_gather | solution.py:14
  215.1 57.5 %all_gather.19 = f32[128,2,8,64]{3,2,1,0:T(8,128)S(1)} all-gather(f32[4,2,8,64]{3,2,1,0:T(8,128)S(1)} %bitcast.267), channel_id=1, replica_groups=mesh['groups'=2,'row'=32,'col'=4,'chan'=2] {'row'}, dimensions={0}, use_global_device_ids=true | all-gather | bytes 540672 | tf_op jit(solution)/shard_map/all_gather | solution.py:14
  272.6 0.3 fusion.19
  272.9 0.4 fusion.15
  273.4 4.0 all_to_all.20
  277.5 0.3 fusion.25
  277.9 106.1 %all-reduce = (f32[128,2]{0,1:T(2,128)S(1)}, f32[64,128]{1,0:T(8,128)S(1)}) all-reduce(f32[128,2]{0,1:T(2,128)S(1)} %fusion.19, f32[64,128]{1,0:T(8,128)S(1)} %fusion.18), channel_id=1, replica_groups=mesh['groups'=2,'row'=32,'col'=4,'chan'=2] {'row'}, use_global_device_ids=true, to_apply=%region_16.17 | all-reduce | flops 8448 | bytes 67584 | tf_op jit(solution)/shard_map/psum | solution.py:41
  384.0 16.2 %all-reduce.1 = (f32[128,2]{0,1:T(2,128)}, f32[64,128]{1,0:T(8,128)}) all-reduce(f32[128,2]{0,1:T(2,128)S(1)} %get-tuple-element.348, f32[64,128]{1,0:T(8,128)S(1)} %get-tuple-element.349), channel_id=1, replica_groups=mesh['groups'=2,'row'=32,'col'=4,'chan'=2] {'col'}, use_global_device_ids=true, to_apply=%region_17.18 | all-reduce | flops 8448 | bytes 67584 | tf_op jit(solution)/shard_map/psum | solution.py:41
  400.2 40.1 %all-reduce.5.cloned.1.call-done = f32[4,128,64]{1,2,0:T(8,128)} async-done(((f32[4,128,64]{1,2,0:T(8,128)}), f32[4,128,64]{1,2,0:T(8,128)}) %all-reduce.5.cloned.1.call-update) | async-done | bytes 131088 | tf_op jit(solution)/shard_map/psum | solution.py:41
  440.4 1.0 fusion.28
  441.4 65.7 %all-reduce.7.cloned.1.call-done = f32[4,128,64]{1,2,0:T(8,128)} async-done(((f32[4,128,64]{1,2,0:T(8,128)}), f32[4,128,64]{1,2,0:T(8,128)}) %all-reduce.7.cloned.1.call-update) | async-done | bytes 131088 | tf_op jit(solution)/shard_map/psum | solution.py:41
  507.1 1.6 copy.166
  (99 shorter events, 4.5 us)
Async XLA Ops:
  7.2 2.3 copy-start
  7.2 1.9 copy-start.2
  25.5 1.0 copy-start.1
  26.4 0.7 copy-start.15
  140.4 0.7 copy-start.5
  140.6 1.0 slice-start
  140.6 1.1 copy-start.4
  141.1 0.8 copy-start.3
  144.9 0.9 copy-start.12
  145.0 1.1 copy-start.6
  145.1 0.9 copy-start.9
  146.1 0.6 copy-start.10
  146.1 0.7 copy-start.13
  146.8 0.8 copy-start.7
  150.7 0.9 copy-start.12
  150.7 1.1 copy-start.6
  150.9 0.9 copy-start.9
  151.8 0.6 copy-start.10
  151.8 0.7 copy-start.13
  152.5 0.8 copy-start.7
  153.3 4.2 copy-start.8
  154.1 5.0 all-to-all-start
  159.1 14.1 %all-to-all-start.1 = ((bf16[4,8,64,128]{3,2,1,0:T(8,128)(2,1)}), bf16[4,8,64,128]{3,2,1,0:T(8,128)(2,1)S(1)}, u32[]{:S(2)}, u32[]{:S(2)}) async-start(bf16[4,8,64,128]{3,2,1,0:T(8,128)(2,1)} %copy.92), calls=%async_computation.1 | async-start | bytes 1048576 | tf_op jit(solution)/shard_map/all_to_all | solution.py:25
  164.3 1.1 copy-start.14
  165.5 0.9 copy-start.11
  173.2 29.7 %all-to-all-start.2 = ((bf16[32,2,512]{2,1,0:T(2,128)(2,1)}), bf16[32,2,512]{2,1,0:T(2,128)(2,1)S(1)}, u32[]{:S(2)}, u32[]{:S(2)}) async-start(bf16[32,2,512]{2,1,0:T(2,128)(2,1)} %reshape.180), calls=%async_computation.2 | async-start | bytes 131072 | tf_op jit(solution)/shard_map/all_to_all | solution.py:25
  178.5 261.9 %all-reduce.5.cloned.1.call-start = ((), (), s32[]{:S(2)}) async-start(), calls=%async_computation.4 | async-start | bytes 262144 | tf_op jit(solution)/shard_map/psum | solution.py:41
  179.9 327.2 %all-reduce.7.cloned.1.call-start = ((), (), s32[]{:S(2)}) async-start(), calls=%async_computation.5 | async-start | bytes 262144 | tf_op jit(solution)/shard_map/psum | solution.py:41
Sparse Core Ops, SparseCore 0:
  182.2 258.0 all-reduce.4
  442.7 64.4 all-reduce.6
where the time goes:
time: 516 us
  blocking collectives  324 us (63%)
  waiting for transfers between devices  136 us (26%)
  local copies, waits for them, and re-layouts  15.9 us (3%)
  between operations  14.4 us (3%)
  starting transfers between devices  13.2 us (3%)
  matrix products  6.9 us (1%)
    all_gather x4, blocking collectives, gathered_by_axis(): value = lax.all_gather(value, axis, axis=dim, tiled=True)  182 us
    psum x2, blocking collectives, one_axis_at_a_time(): return functools.reduce(lax.psum, axes, value)  122 us
    psum x2, waiting for transfers between devices, one_axis_at_a_time(): return functools.reduce(lax.psum, axes, value)  106 us
    all_to_all x2, waiting for transfers between devices, sent_and_summed(): lax.all_to_all(cut_along(value, dim, length), axis, 0, 0, tiled=True)  29.1 us
    all_gather x1, blocking collectives, sent_together(): lax.all_gather(both, axis, axis=dim, tiled=True)  15.4 us
  transfers between devices with their start and end apart: 5, of which 5 were waited for; matrix products, arithmetic and copies ran while one was open for 2% of the time, Pallas kernels for 0%

commit v1 on v0

v1 whole, which is shorter than its diff:
```python
import functools

import jax
import jax.numpy as jnp
from jax import lax
from jax.experimental import pallas as pl
from jax.experimental.pallas import tpu as pltpu
from jax.sharding import PartitionSpec as P

EPSILON = 1e-05
MASK_BIG = 1000000000.0
MESH = pl.DeviceIdType.MESH
F32 = jnp.float32
BF16 = jnp.bfloat16
HOP = 4
DMA = pltpu.SemaphoreType.DMA


def place(axis, step):
    size = lax.axis_size(axis)
    return lax.rem(lax.axis_index(axis) + (step % size), size)


def remote(src, dst, send, recv, axis, step):
    return pltpu.make_async_remote_copy(
        src_ref=src,
        dst_ref=dst,
        send_sem=send,
        recv_sem=recv,
        device_id={axis: place(axis, step)},
        device_id_type=MESH,
    )


def arrived(dst, recv):
    pltpu.make_async_copy(dst, dst, recv).wait()


def meet(chan):
    barrier = pltpu.get_barrier_semaphore()
    steps = [("row", s * t) for t in range(1, HOP + 1) for s in (1, -1)]
    steps += [("col", d) for d in range(1, lax.axis_size("col"))]
    if chan:
        steps += [("chan", 1)]
    for axis, step in steps:
        pl.semaphore_signal(
            barrier, inc=1, device_id={axis: place(axis, step)}, device_id_type=MESH
        )
    pl.semaphore_wait(barrier, len(steps))


def gather_everywhere(piece, out, zs, zr, xs, xr, beside):
    length, width = lax.axis_size("row"), lax.axis_size("col")
    x, half = lax.axis_index("col"), length // 2
    last = half // HOP

    def along_row(src, delta, steps):
        slot = out.at[x, place("row", -delta)]
        for step in steps:
            remote(src, slot, zs, zr.at[(delta + step) % length], "row", step).start()

    def along_col(src, delta):
        slot = out.at[x, place("row", -delta)]
        for d in range(1, width):
            remote(src, slot, xs, xr.at[d], "col", d).start()

    def slot_of(delta):
        return out.at[x, place("row", -delta)]

    along_row(piece, 0, [s * t for t in (HOP, 3, 2, 1) for s in (1, -1)])
    beside()
    along_col(piece, 0)
    out[x, lax.axis_index("row")] = piece[...]
    for a in range(1, last + 1):
        for s in (1, -1):
            if a == last:
                continue
            delta = s * HOP * a
            arrived(slot_of(delta), zr.at[delta % length])
            far = [s * HOP] if (s == 1 or a < last - 1) else []
            along_row(slot_of(delta), delta, far + [s * t for t in (3, 2, 1)])
        for s in (1, -1):
            if a < last:
                along_col(slot_of(s * HOP * a), s * HOP * a)
            for t in range(1, HOP):
                delta = s * (HOP * (a - 1) + t)
                arrived(slot_of(delta), zr.at[delta % length])
                along_col(slot_of(delta), delta)
    arrived(slot_of(half), zr.at[half])
    along_col(slot_of(half), half)
    for d in range(1, width):
        arrived(out.at[place("col", -d)], xr.at[d])
    rest = out.at[0, pl.ds(0, length - 1)]
    arrived(rest, zs)
    rest = out.at[pl.ds(0, width - 1)]
    arrived(rest, xs)


def exchange(src, dst, xs, xr):
    for d in range(1, lax.axis_size("col")):
        remote(
            src.at[place("col", d)], dst.at[lax.axis_index("col")], xs, xr.at[d], "col", d
        ).start()


def exchanged(dst, xs, xr):
    for d in range(1, lax.axis_size("col")):
        arrived(dst.at[place("col", -d)], xr.at[d])
    arrived(dst.at[pl.ds(0, lax.axis_size("col") - 1)], xs)


def gather_kernel(piece, tile, cot, mask, out, rows, cots, masks, zs, zr, xs, xr, es, er):
    meet(False)
    x = lax.axis_index("col")

    def beside():
        pairs = ((tile, rows), (cot, cots), (mask, masks))
        for n, (src, dst) in enumerate(pairs):
            exchange(src, dst, es.at[n], er.at[n])
        for src, dst in pairs:
            dst[x] = src[x]

    gather_everywhere(piece, out, zs, zr, xs, xr, beside)
    for n, dst in enumerate((rows, cots, masks)):
        exchanged(dst, es.at[n], er.at[n])


def over(a, b):
    return lax.dot_general(a, b, (((1,), (1,)), ((), ())), preferred_element_type=F32)


def under(a, b):
    return lax.dot_general(a, b, (((0,), (0,)), ((), ())), preferred_element_type=F32)


def plain(a, b):
    return lax.dot_general(a, b, (((1,), (0,)), ((), ())), preferred_element_type=F32)


def attend_kernel(
    scale, bias, rows, cots, masks, wqk, wvg, wout, d_bias, upd, dn, grads
):
    width, row_count, block, channels = rows.shape
    tokens = width * block
    cols = wout.shape[0]
    size = cols // 2
    head_lane = lax.broadcasted_iota(jnp.int32, (block, cols), 1) < size
    lane = lax.broadcasted_iota(jnp.int32, (tokens, 2 * block), 1) < block
    lane_col = lax.broadcasted_iota(jnp.int32, (tokens, cols), 1) < size
    span = 2 * block

    def doubled(values):
        parts = []
        for n in range(width):
            part = values[n * block : (n + 1) * block]
            zero = jnp.zeros_like(part)
            parts += [jnp.where(head_lane, part, zero), jnp.where(head_lane, zero, part)]
        return jnp.concatenate(parts, 0)

    def halved(values):
        parts = []
        for n in range(width):
            first = values[n * span : n * span + block]
            second = values[n * span + block : (n + 1) * span]
            parts += [jnp.where(head_lane, first, second)]
        return jnp.concatenate(parts, 0)

    def per_head(parts, joined, reduced, empty):
        both = functools.reduce(joined, parts)
        first = reduced(jnp.where(lane, both, empty), axis=1, keepdims=True)
        second = reduced(jnp.where(lane, empty, both), axis=1, keepdims=True)
        return jnp.where(lane, first, second)

    bias_sum = [None] * width
    gqk = gvg = gout = None
    for r in range(row_count):
        normed = rows[:, r].reshape(tokens, channels)
        cot = cots[:, r].reshape(tokens, channels)
        qk = plain(normed, wqk[...])
        vg = plain(normed, wvg[...])
        query = (qk[:, :cols] * scale).astype(BF16)
        key2 = doubled(qk[:, cols:]).astype(BF16)
        value2 = doubled(vg[:, :cols]).astype(BF16)
        gate = jax.nn.sigmoid(vg[:, cols:])
        scores = over(query, key2)
        parts = [
            (scores[:, n * span : (n + 1) * span] + bias[n]) + masks[n, r : r + 1, :]
            for n in range(width)
        ]
        top = per_head(parts, jnp.maximum, jnp.max, -jnp.inf)
        parts = [jnp.exp(part - top) for part in parts]
        inverse = 1.0 / per_head(parts, jnp.add, jnp.sum, 0.0)
        weights = [part * inverse for part in parts]
        weights_b = jnp.concatenate([w.astype(BF16) for w in weights], 1)
        attended = plain(weights_b, value2)
        gated = (gate * attended).astype(BF16)
        upd[:, r] = plain(gated, wout[...]).astype(BF16).reshape(width, block, channels)
        d_gated = over(cot, wout[...])
        d_gate = d_gated * attended * gate * (1.0 - gate)
        d_attended = (d_gated * gate).astype(BF16)
        d_weights = over(d_attended, value2)
        product = d_attended.astype(F32) * attended
        first = jnp.sum(jnp.where(lane_col, product, 0.0), axis=1, keepdims=True)
        second = jnp.sum(jnp.where(lane_col, 0.0, product), axis=1, keepdims=True)
        row_dot = jnp.where(lane, first, second)
        d_scores = [
            weights[n] * (d_weights[:, n * span : (n + 1) * span] - row_dot)
            for n in range(width)
        ]
        bias_sum = [d if b is None else b + d for b, d in zip(bias_sum, d_scores)]
        d_scores_b = jnp.concatenate([d.astype(BF16) for d in d_scores], 1)
        d_query = plain(d_scores_b, key2) * scale
        d_key = halved(under(d_scores_b, query))
        d_value = halved(under(weights_b, d_attended))
        dqk = jnp.concatenate([d_query, d_key], 1).astype(BF16)
        dvg = jnp.concatenate([d_value, d_gate], 1).astype(BF16)
        back = over(dqk, wqk[...]) + over(dvg, wvg[...])
        dn[:, r] = back.astype(BF16).reshape(width, block, channels)
        new = (under(normed, dqk), under(normed, dvg), under(gated, cot))
        if gqk is None:
            gqk, gvg, gout = new
        else:
            gqk, gvg, gout = gqk + new[0], gvg + new[1], gout + new[2]
    for n in range(width):
        d_bias[n] = bias_sum[n].astype(BF16)
    share = grads.shape[1]
    everything = jnp.concatenate([gqk, gvg, gout], 0).astype(BF16)
    for n in range(width):
        grads[n] = everything[n * share : (n + 1) * share]


def reduce_kernel(
    d_bias, grads, upd, dn, standard, inverse, w_bias, update, grad, final,
    bias_in, grads_in, upd_in, dn_in, upd_other, dn_mine, dn_other, pieces, plus, minus,
    acc_plus, acc_minus, send_plus, send_minus, piece, xs, xr, ls, lp, lm, ap, am, rs, cs, cr,
    gzs, gzr, gxs, gxr,
):
    length, width = lax.axis_size("row"), lax.axis_size("col")
    x, z = lax.axis_index("col"), lax.axis_index("row")
    half = length // 2
    chain = half // HOP
    row_count = d_bias.shape[1] // length
    meet(True)
    sources = ((d_bias, bias_in), (grads, grads_in), (upd, upd_in), (dn, dn_in))
    for n, (src, dst) in enumerate(sources):
        exchange(src, dst, xs.at[n], xr.at[n])
    for src, dst in sources:
        dst[x] = src[x]
    exchanged(bias_in, xs.at[0], xr.at[0])
    exchanged(grads_in, xs.at[1], xr.at[1])
    total = jnp.sum(bias_in[...].astype(F32), 0).reshape(length, row_count, -1)
    share = jnp.sum(grads_in[...].astype(F32), 0).reshape(-1, HOP, total.shape[-1])
    used = share.shape[0]
    share = jnp.concatenate(
        [share, jnp.zeros((length - used,) + share.shape[1:], F32)], 0
    )
    blank = jnp.zeros((length, pieces.shape[1] - row_count - HOP, total.shape[-1]), F32)
    pieces[...] = jnp.concatenate([total, share, blank], 1).astype(BF16)

    sides = ((1, plus, acc_plus, send_plus, lp, ap), (-1, minus, acc_minus, send_minus, lm, am))
    for a in range(chain - 1, -1, -1):
        for s, leaves, acc, _, leaf_sem, acc_sem in sides:
            if s == 1 and a == chain - 1:
                remote(
                    pieces.at[place("row", -half)], acc.at[a], ls, acc_sem.at[a], "row", -HOP
                ).start()
            for t in range(HOP - 1, 0, -1):
                remote(
                    pieces.at[place("row", -s * (t + HOP * a))],
                    leaves.at[a, t - 1],
                    ls,
                    leaf_sem.at[a],
                    "row",
                    -s * t,
                ).start()
    exchanged(upd_in, xs.at[2], xr.at[2])
    other = remote(upd_in, upd_other, cs.at[0], cr.at[0], "chan", 1)
    other.start()
    exchanged(dn_in, xs.at[3], xr.at[3])
    for a in range(chain - 1, 0, -1):
        for s, leaves, acc, out, leaf_sem, acc_sem in sides:
            arrived(leaves.at[a], leaf_sem.at[a])
            value = pieces[place("row", -s * HOP * a)].astype(F32)
            value = value + jnp.sum(leaves[a].astype(F32), 0)
            if s == 1 or a < chain - 1:
                arrived(acc.at[a], acc_sem.at[a])
                value = value + acc[a].astype(F32)
            out[a] = value.astype(BF16)
            remote(out.at[a], acc.at[a - 1], rs, acc_sem.at[a - 1], "row", -s * HOP).start()
        if a == chain - 1:
            other.wait()
            update[...] = (upd_in[...].astype(F32) + upd_other[...].astype(F32)).astype(BF16)
    value = pieces[z].astype(F32)
    for s, leaves, acc, out, leaf_sem, acc_sem in sides:
        arrived(leaves.at[0], leaf_sem.at[0])
        arrived(acc.at[0], acc_sem.at[0])
        value = value + jnp.sum(leaves[0].astype(F32), 0) + acc[0].astype(F32)
    tile = value[:row_count]
    columns = jnp.transpose(tile)
    block = columns.shape[0] // 2
    sums = [None, None]
    for j in range(row_count):
        normed = standard[j // 2, j % 2].astype(BF16).astype(F32)
        added = dn_in[j // 2, j % 2].astype(F32)
        for h in range(2):
            column = columns[h * block : (h + 1) * block, j : j + 1]
            added = added + column * w_bias[h : h + 1, :]
            term = normed * column
            sums[h] = term if sums[h] is None else sums[h] + term
        dn_mine[j // 2, j % 2] = added.astype(BF16)
    sums = [jnp.sum(term, 0, keepdims=True) for term in sums]
    blank = jnp.zeros((piece.shape[0] - HOP - 2, tile.shape[-1]), F32)
    piece[...] = jnp.concatenate([value[row_count : row_count + HOP], *sums, blank], 0)

    def beside():
        other = remote(dn_mine, dn_other, cs.at[1], cr.at[1], "chan", 1)
        other.start()
        other.wait()
        d_total = dn_mine[...].astype(F32) + dn_other[...].astype(F32)
        normal = standard[...]
        centred = d_total - jnp.mean(d_total, -1, keepdims=True)
        centred = centred - normal * jnp.mean(d_total * normal, -1, keepdims=True)
        grad[...] = (inverse[...] * centred).astype(BF16)

    gather_everywhere(piece, final, gzs, gzr, gxs, gxr, beside)
    arrived(pieces.at[pl.ds(0, 2 * (HOP - 1) * chain + 1)], ls)
    arrived(pieces.at[pl.ds(0, 2 * (chain - 1))], rs)


def call(kernel, name, identity, outs, scratch, *args):
    params = dict(vmem_limit_bytes=24 * 2**20)
    if identity is not None:
        params.update(collective_id=identity, has_side_effects=True)
    vmem = pl.BlockSpec(memory_space=pltpu.VMEM)
    return pl.pallas_call(
        kernel,
        out_shape=[jax.ShapeDtypeStruct(shape, kind) for shape, kind in outs],
        in_specs=[vmem] * len(args),
        out_specs=[vmem] * len(outs),
        scratch_shapes=scratch,
        compiler_params=pltpu.CompilerParams(**params),
        name=name,
    )(*args)


def on_device(pair_rep, pair_mask, w_qkvg, w_bias, w_out, cotangent):
    full_rows, block, channels = pair_rep.shape
    length, width = lax.axis_size("row"), lax.axis_size("col")
    cols = w_qkvg.shape[2]
    heads = w_bias.shape[1]
    scale = (cols // heads) ** (-0.5)
    own = full_rows // width
    tokens = width * block
    span = heads * block
    values = pair_rep.astype(F32)
    centred = values - jnp.mean(values, -1, keepdims=True)
    inverse = lax.rsqrt(jnp.mean(centred * centred, -1, keepdims=True) + EPSILON)
    standard = centred * inverse
    normed = standard.astype(BF16)
    piece = jnp.einsum("ijc,ch->ihj", normed, w_bias, preferred_element_type=F32)
    piece = piece.reshape(full_rows, span)
    mask = MASK_BIG * (pair_mask.astype(F32) - 1.0)
    mask = jnp.concatenate([mask, mask], 1).reshape(width, own, span)
    mask = jnp.pad(mask, ((0, 0), (0, 8 - own), (0, 0)))
    tiled = (width, own, block, channels)
    gathered = (width, length, full_rows, span)
    across = [DMA, DMA((length,)), DMA, DMA((width,))]
    bias, rows, cots, masks = call(
        gather_kernel,
        "gather",
        0,
        [(gathered, F32), (tiled, BF16), (tiled, BF16), (mask.shape, F32)],
        across + [DMA((3,)), DMA((3, width))],
        piece,
        normed.reshape(tiled),
        cotangent.reshape(tiled),
        mask,
    )
    wqk = jnp.concatenate([w_qkvg[0], w_qkvg[1]], 1)
    wvg = jnp.concatenate([w_qkvg[2], w_qkvg[3]], 1)
    grad_rows = 2 * channels + cols
    d_bias, upd, dn, grads = call(
        functools.partial(attend_kernel, scale),
        "attend",
        None,
        [
            ((width, tokens, span), BF16),
            (tiled, BF16),
            (tiled, BF16),
            ((width, grad_rows // width, channels), BF16),
        ],
        [],
        bias.reshape(width, tokens, span),
        rows,
        cots,
        masks,
        wqk,
        wvg,
        w_out,
    )
    V = pltpu.VMEM
    chain = length // 2 // HOP
    message = (2 * full_rows, span)
    tile, share = (V(tiled, BF16), V(grads.shape, BF16))
    relays = [V((chain, HOP - 1) + message, BF16)] * 2 + [V((chain,) + message, BF16)] * 4
    update, grad, final = call(
        reduce_kernel,
        "reduce",
        1,
        [(tiled, BF16), (tiled, BF16), (gathered, F32)],
        [V(d_bias.shape, BF16), share, tile, tile, tile, tile, tile]
        + [V((length,) + message, BF16)]
        + relays
        + [V((full_rows, span), F32)]
        + [DMA((4,)), DMA((4, width)), DMA]
        + [DMA((chain,))] * 4
        + [DMA, DMA((2,)), DMA((2,))]
        + across,
        d_bias,
        grads,
        upd,
        dn,
        standard.reshape(tiled),
        inverse.reshape(width, own, block, 1),
        w_bias.astype(F32).T,
    )
    used = grad_rows // width // HOP
    sums = final[:, :used, :HOP].reshape(grad_rows, channels) / tokens
    qkvg = sums[: 2 * channels].reshape(2, channels, 2, cols).transpose(0, 2, 1, 3)
    bias_grad = jnp.sum(final[:, :, HOP : HOP + heads], (0, 1)).T / tokens
    shape = pair_rep.shape
    return (
        update.reshape(shape),
        grad.reshape(shape),
        qkvg.reshape(w_qkvg.shape),
        bias_grad,
        sums[2 * channels :],
    )


def solution(mesh):
    in_specs = (
        P(("groups", "row"), "col", None),
        P(("groups", "row"), "col"),
        P(None, None, "chan"),
        P(None, "chan"),
        P("chan", None),
        P(("groups", "row"), "col", None),
    )
    out_specs = (
        P(("groups", "row"), "col", None),
        P(("groups", "row"), "col", None),
        P("groups", None, "chan"),
        P("groups", "chan"),
        P("chan", "groups"),
    )
    return jax.shard_map(
        on_device, mesh=mesh, in_specs=in_specs, out_specs=out_specs, check_vma=False
    )
```

time: 516 us -> 132 us (0.26)
  blocking collectives: 324 us -> 0 us
  waiting for transfers between devices: 136 us -> 0 us
  Pallas kernels: 0 us -> 123 us
  between operations: 14.4 us -> 0.82 us
  starting transfers between devices: 13.2 us -> 0 us
  local copies, waits for them, and re-layouts: 15.9 us -> 5.18 us
  matrix products: 6.9 us -> 0.2 us
    all_gather x5 -> x0, blocking collectives: 198 us -> none  [the longest x4 182 us: gathered_by_axis(): value = lax.all_gather(value, axis, axis=dim, tiled=True)]
    pallas_call x0 -> x3, Pallas kernels: none -> 123 us  [call(): pl.pallas_call(kernel, out_shape=[jax.ShapeDtypeStruct(shape, kind) for s...]
    psum x2 -> x0, blocking collectives: 122 us -> none  [one_axis_at_a_time(): return functools.reduce(lax.psum, axes, value)]
    psum x2 -> x0, waiting for transfers between devices: 106 us -> none  [one_axis_at_a_time(): return functools.reduce(lax.psum, axes, value)]
    all_to_all x3 -> x0, waiting for transfers between devices: 29.8 us -> none  [the longest x2 29.1 us: sent_and_summed(): lax.all_to_all(cut_along(value, dim, length), axis, 0, 0, tiled=True)]
    all_to_all x3 -> x0, starting transfers between devices: 13 us -> none  [the longest x2 9.56 us: sent_and_summed(): lax.all_to_all(cut_along(value, dim, length), axis, 0, 0, tiled=True)]
    dot_general x21 -> x1, matrix products: 6 us -> 0.2 us  [on_device(): jnp.einsum('ijc,ch->ihj', normed, w_bias, preferred_element_type=F32)]
  transfers between devices with their start and end apart: 5 -> 0, of which waited for: 5 -> 0; matrix products, arithmetic and copies ran while one was open for 2% -> 0% of each run, Pallas kernels for 0% -> 0%
where the time goes in v1:
time: 132 us; the launch traced here: 131 us
  Pallas kernels  123 us (93%)
  local copies, waits for them, and re-layouts  5.18 us (4%)
  other arithmetic  2.5 us (2%)
    pallas_call x3, Pallas kernels, call(): pl.pallas_call(kernel, out_shape=[jax.ShapeDtypeStruct(shape, kind) for s...  123 us
    unnamed x18, local copies, waits for them, and re-layouts  3.47 us

profile of v1, /device:TPU:40, one launch (start us, length us, event | category | flops | bytes accessed | tf_op | source)
XLA Modules:
  0.0 131.3 jit_solution(11390259698268234627)
XLA Ops:
  0.6 0.0 copy-start.2
  0.6 1.1 convert_reduce_fusion
  1.8 0.0 copy-done.2
  1.8 0.3 fusion.2
  2.1 0.0 copy-start.5
  2.1 0.2 fusion
  2.3 0.0 copy-start
  2.3 0.4 copy-done.5
  2.7 0.2 convolution_bitcast_fusion
  2.9 0.0 copy-start.4
  2.9 0.1 reshape.77.piece
  3.0 0.6 copy-done.4
  3.6 0.1 pad_maximum_fusion.2
  3.7 0.0 copy-done
  3.7 0.0 copy-start.3
  3.7 66.9 %gather.1 = (f32[4,32,8,128]{3,2,1,0:T(8,128)S(1)}, bf16[4,2,64,128]{3,2,1,0:T(8,128)(2,1)S(1)}, bf16[4,2,64,128]{3,2,1,0:T(8,128)(2,1)S(1)}, f32[4,8,128]{2,1,0:T(8,128)S(1)}) custom-call(f32[8,128]{1,0:T(8,128)S(1)} %reshape.77.piece, bf16[4,2,64,128]{3,2,1,0:T(8,128)(2,1)S(1)} %bitcast.27, bf16[4,2,64,128]{3,2,1,0:T(8,128)(2,1)S(1)} %bitcast.30, ...), custom_call_target="tpu_custom_call" | custom-call | tf_op jit(solution)/shard_map/gather/pallas_call | solution.py:335
  70.7 0.0 copy-done.3
  70.7 0.1 copy.29
  70.8 0.1 copy.30
  70.9 0.1 copy.31
  71.1 0.1 copy.32
  71.2 0.0 copy-start.1
  71.2 0.1 pad_maximum_fusion
  71.3 0.6 copy-done.1
  71.9 3.1 %attend.1 = (bf16[4,256,128]{2,1,0:T(8,128)(2,1)S(1)}, bf16[4,2,64,128]{3,2,1,0:T(8,128)(2,1)S(1)}, bf16[4,2,64,128]{3,2,1,0:T(8,128)(2,1)S(1)}, bf16[4,80,128]{2,1,0:T(8,128)(2,1)S(1)}) custom-call(f32[4,256,128]{2,1,0:T(8,128)S(1)} %bitcast.29, bf16[4,2,64,128]{3,2,1,0:T(8,128)(2,1)S(1)} %get-tuple-element.17.rows, ...), custom_call_target="tpu_custom_call" | custom-call | tf_op jit(solution)/shard_map/attend/pallas_call | solution.py:335
  75.0 0.1 copy.26.inverse
  75.1 52.6 %reduce.1 = (bf16[4,2,64,128]{3,2,1,0:T(8,128)(2,1)S(1)}, bf16[4,2,64,128]{3,2,1,0:T(8,128)(2,1)S(1)}, f32[4,32,8,128]{3,2,1,0:T(8,128)S(1)}) custom-call(bf16[4,256,128]{2,1,0:T(8,128)(2,1)S(1)} %get-tuple-element.20.d_bias, bf16[4,80,128]{2,1,0:T(8,128)(2,1)S(1)} %get-tuple-element.21.grads, bf16[4,2,64,128]{3,2,1,0:T(8,128)(2,1)S(1)} %get-tuple-element.22.upd, ...), custom_call_target="tpu_custom_call" | custom-call | tf_op jit(solution)/shard_map/reduce/pallas_call | solution.py:335
  127.8 0.1 copy.27
  127.9 0.1 reshape.85
  128.0 0.7 copy.28
  128.6 0.6 slice.33
  129.3 0.1 slice_reduce_fusion
  129.4 0.6 multiply_bitcast_fusion
  130.0 0.7 copy.35
  130.6 0.7 copy.36
  (8 shorter events, 0.1 us)
Async XLA Ops:
  0.6 1.1 copy-start.2
  2.1 0.7 copy-start.5
  2.3 1.4 %copy-start = (bf16[8,64,128]{2,1,0:T(8,128)(2,1)S(1)}, bf16[8,64,128]{2,1,0:T(8,128)(2,1)}, u32[]{:S(2)}) copy-start(bf16[8,64,128]{2,1,0:T(8,128)(2,1)} %param.11) | copy-start | bytes 393220
  2.9 0.7 copy-start.4
  3.7 67.0 %copy-start.3 = (bf16[4,128,64]{1,2,0:T(8,128)(2,1)S(1)}, bf16[4,128,64]{1,2,0:T(8,128)(2,1)}, u32[]{:S(2)}) copy-start(bf16[4,128,64]{1,2,0:T(8,128)(2,1)} %param.8) | copy-start | bytes 196612
  71.2 0.7 copy-start.1

commit v2 on v1

v2 whole, which is shorter than its diff:
```python
import functools

import jax
import jax.numpy as jnp
from jax import lax
from jax.experimental import pallas as pl
from jax.experimental.pallas import tpu as pltpu
from jax.sharding import PartitionSpec as P

EPSILON = 1e-05
MASK_BIG = 1000000000.0
MESH = pl.DeviceIdType.MESH
F32 = jnp.float32
BF16 = jnp.bfloat16
HOP = 4
DMA = pltpu.SemaphoreType.DMA


def place(axis, step):
    size = lax.axis_size(axis)
    return lax.rem(lax.axis_index(axis) + (step % size), size)


def remote(src, dst, send, recv, axis, step):
    return pltpu.make_async_remote_copy(
        src_ref=src,
        dst_ref=dst,
        send_sem=send,
        recv_sem=recv,
        device_id={axis: place(axis, step)},
        device_id_type=MESH,
    )


def arrived(dst, recv):
    pltpu.make_async_copy(dst, dst, recv).wait()


def gather_everywhere(piece, out, zs, zr, xs, xr, beside):
    length, width = lax.axis_size("row"), lax.axis_size("col")
    x, half = lax.axis_index("col"), length // 2
    last = half // HOP

    def slot_of(delta):
        return out.at[x, place("row", -delta)]

    def along_row(src, delta, steps):
        for step in steps:
            recv = zr.at[(delta + step) % length]
            remote(src, slot_of(delta), zs, recv, "row", step).start()

    def along_col(src, delta):
        for d in range(1, width):
            remote(src, slot_of(delta), xs, xr.at[d], "col", d).start()

    along_row(piece, 0, [s * t for t in (HOP, 3, 2, 1) for s in (1, -1)])
    along_col(piece, 0)
    out[x, lax.axis_index("row")] = piece[...]
    result = beside()
    for a in range(1, last + 1):
        for s in (1, -1):
            if a == last:
                continue
            delta = s * HOP * a
            arrived(slot_of(delta), zr.at[delta % length])
            far = [s * HOP] if (s == 1 or a < last - 1) else []
            along_row(slot_of(delta), delta, far + [s * t for t in (3, 2, 1)])
        for s in (1, -1):
            if a < last:
                along_col(slot_of(s * HOP * a), s * HOP * a)
            for t in range(1, HOP):
                delta = s * (HOP * (a - 1) + t)
                arrived(slot_of(delta), zr.at[delta % length])
                along_col(slot_of(delta), delta)
    arrived(slot_of(half), zr.at[half])
    along_col(slot_of(half), half)
    for d in range(1, width):
        arrived(out.at[place("col", -d)], xr.at[d])
    arrived(out.at[0, pl.ds(0, length - 1)], zs)
    arrived(out.at[pl.ds(0, width - 1)], xs)
    return result


def by_distance(length):
    return [s * t for t in range(1, length // 2) for s in (1, -1)] + [length // 2]


def to_all_rows(src_of, dst, send, recv_of):
    for step in reversed(by_distance(lax.axis_size("row"))):
        remote(src_of(step), dst, send, recv_of(step), "row", step).start()


def exchange(src, dst, xs, xr):
    for d in range(1, lax.axis_size("col")):
        remote(
            src.at[place("col", d)], dst.at[lax.axis_index("col")], xs, xr.at[d], "col", d
        ).start()


def exchanged(dst, xs, xr):
    for d in range(1, lax.axis_size("col")):
        arrived(dst.at[place("col", -d)], xr.at[d])
    arrived(dst.at[pl.ds(0, lax.axis_size("col") - 1)], xs)


def over(a, b):
    return lax.dot_general(a, b, (((1,), (1,)), ((), ())), preferred_element_type=F32)


def under(a, b):
    return lax.dot_general(a, b, (((0,), (0,)), ((), ())), preferred_element_type=F32)


def plain(a, b):
    return lax.dot_general(a, b, (((1,), (0,)), ((), ())), preferred_element_type=F32)


def standardized(values):
    values = values.astype(F32)
    centred = values - jnp.mean(values, -1, keepdims=True)
    inverse = lax.rsqrt(jnp.mean(centred * centred, -1, keepdims=True) + EPSILON)
    return centred * inverse, inverse


def add_up(values):
    return functools.reduce(jnp.add, values)


def whole_kernel(
    scale, pair, cot, mask, w_qkvg, w_bias, w_out, update, grad, share_all, bias_all,
    piece, bias, rows, cots, mask_own, masks, d_bias, bias_in, upd, upd_in, upd_other,
    dn, dn_in, dn_mine, dn_other, grads, grads_in, pieces, plus, minus, acc_plus, acc_minus,
    send_plus, send_minus, shares, shares_in, share_own, bias_own, bias_x, bias_row,
    gzs, gzr, gxs, gxr, es, er, bs, br, ls, lp, lm, ap, am, rs, cs, cr, ss, sr, fs, fr, fxs, fxr,
    ws, wr, vs, vr,
):
    length, width = lax.axis_size("row"), lax.axis_size("col")
    x, z = lax.axis_index("col"), lax.axis_index("row")
    _, row_count, block, channels = pair.shape
    cols = w_out.shape[0]
    size = cols // 2
    tokens, span, half = width * block, 2 * block, length // 2
    chain = half // HOP
    full_rows = width * row_count
    steps = [("chan", 1)] + [("col", d) for d in range(1, width)]
    steps += [("row", s * t) for t in range(1, HOP + 1) for s in (1, -1)]
    barrier = pltpu.get_barrier_semaphore()
    for axis, step in steps:
        pl.semaphore_signal(
            barrier, inc=1, device_id={axis: place(axis, step)}, device_id_type=MESH
        )

    standard, inverse = standardized(pair[...].reshape(full_rows * block, channels))
    normed_own = standard.astype(BF16)
    line = lax.broadcasted_iota(jnp.int32, (channels, channels), 0)
    eye = (line == lax.broadcasted_iota(jnp.int32, (channels, channels), 1)).astype(BF16)
    w_rows = under(w_bias[...], eye)
    flat = over(w_rows.astype(BF16), normed_own)
    lines = []
    for j in range(full_rows):
        part = flat[:, j * block : (j + 1) * block]
        lines += [jnp.concatenate([part[0:1], part[1:2]], 1)]
    piece[...] = jnp.concatenate(lines, 0)
    valid = MASK_BIG * (mask[...].astype(F32) - 1.0)
    mask_own[...] = jnp.concatenate([valid, valid], 1)
    wqk = jnp.concatenate([w_qkvg[0], w_qkvg[1]], 1)
    wvg = jnp.concatenate([w_qkvg[2], w_qkvg[3]], 1)
    pl.semaphore_wait(barrier, len(steps))

    head_lane = lax.broadcasted_iota(jnp.int32, (block, cols), 1) < size
    lane = lax.broadcasted_iota(jnp.int32, (tokens, span), 1) < block
    lane_col = lax.broadcasted_iota(jnp.int32, (tokens, cols), 1) < size

    def doubled(values):
        parts = []
        for n in range(width):
            part = values[n * block : (n + 1) * block]
            zero = jnp.zeros_like(part)
            parts += [jnp.where(head_lane, part, zero), jnp.where(head_lane, zero, part)]
        return jnp.concatenate(parts, 0)

    def halved(values):
        parts = []
        for n in range(width):
            first = values[n * span : n * span + block]
            second = values[n * span + block : (n + 1) * span]
            parts += [jnp.where(head_lane, first, second)]
        return jnp.concatenate(parts, 0)

    def per_head(parts, joined, reduced, empty):
        both = functools.reduce(joined, parts)
        first = reduced(jnp.where(lane, both, empty), axis=1, keepdims=True)
        second = reduced(jnp.where(lane, empty, both), axis=1, keepdims=True)
        return jnp.where(lane, first, second)

    def projections():
        exchange(pair, rows, es.at[0], er.at[0])
        exchange(cot, cots, es.at[1], er.at[1])
        for d in range(1, width):
            remote(mask_own, masks.at[x], es.at[2], er.at[2, d], "col", d).start()
        rows[x], cots[x], masks[x] = pair[x], cot[x], mask_own[...]
        for n, dst in enumerate((rows, cots, masks)):
            exchanged(dst, es.at[n], er.at[n])
        result = []
        for r in range(row_count):
            normed = standardized(rows[:, r].reshape(tokens, channels))[0].astype(BF16)
            row_cot = cots[:, r].reshape(tokens, channels)
            qk, vg = plain(normed, wqk), plain(normed, wvg)
            query = (qk[:, :cols] * scale).astype(BF16)
            key2 = doubled(qk[:, cols:]).astype(BF16)
            value2 = doubled(vg[:, :cols]).astype(BF16)
            gate = jax.nn.sigmoid(vg[:, cols:])
            d_gated = over(row_cot, w_out[...])
            d_attended = (d_gated * gate).astype(BF16)
            scores = over(query, key2)
            d_weights = over(d_attended, value2)
            result += [
                (normed, row_cot, query, key2, value2, gate, d_gated, d_attended, scores, d_weights)
            ]
        return result

    known = gather_everywhere(piece, bias, gzs, gzr, gxs, gxr, projections)

    bias_sum = [None] * width
    saved = []
    for r in range(row_count):
        _, _, _, _, value2, _, _, d_attended, scores, d_weights = known[r]
        parts = [
            (scores[:, n * span : (n + 1) * span] + bias[n].reshape(tokens, span))
            + masks[n, pl.ds(x * row_count + r, 1), :]
            for n in range(width)
        ]
        top = per_head(parts, jnp.maximum, jnp.max, -jnp.inf)
        parts = [jnp.exp(part - top) for part in parts]
        below = 1.0 / per_head(parts, jnp.add, jnp.sum, 0.0)
        weights = [part * below for part in parts]
        weights_b = jnp.concatenate([w.astype(BF16) for w in weights], 1)
        attended = plain(weights_b, value2)
        product = d_attended.astype(F32) * attended
        first = jnp.sum(jnp.where(lane_col, product, 0.0), axis=1, keepdims=True)
        second = jnp.sum(jnp.where(lane_col, 0.0, product), axis=1, keepdims=True)
        row_dot = jnp.where(lane, first, second)
        d_scores = [
            weights[n] * (d_weights[:, n * span : (n + 1) * span] - row_dot)
            for n in range(width)
        ]
        bias_sum = [d if b is None else b + d for b, d in zip(bias_sum, d_scores)]
        d_scores_b = jnp.concatenate([d.astype(BF16) for d in d_scores], 1)
        saved += [(weights_b, attended, d_scores_b)]
    for n in range(width):
        d_bias[n] = bias_sum[n].reshape(length, full_rows, span).astype(BF16)
    groups = []
    for a in range(chain):
        group = [s * (HOP * a + t) for t in range(1, HOP) for s in (1, -1)]
        group += [s * HOP * a for s in (1, -1)] if a else [0]
        groups += [group + [half] if a == chain - 1 else group]
    for a in range(chain - 1, -1, -1):
        for delta in groups[a]:
            dest = place("row", -delta)
            for d in range(1, width):
                remote(
                    d_bias.at[place("col", d), dest], bias_in.at[x, dest], bs, br.at[a, d], "col", d
                ).start()
    bias_in[x] = d_bias[x]

    gqk = gvg = gout = None
    for r in range(row_count):
        normed, row_cot, query, key2, _, gate, d_gated, d_attended, _, _ = known[r]
        weights_b, attended, d_scores_b = saved[r]
        gated = (gate * attended).astype(BF16)
        upd[:, r] = plain(gated, w_out[...]).astype(BF16).reshape(width, block, channels)
        d_gate = d_gated * attended * gate * (1.0 - gate)
        d_query = plain(d_scores_b, key2) * scale
        d_key = halved(under(d_scores_b, query))
        d_value = halved(under(weights_b, d_attended))
        dqk = jnp.concatenate([d_query, d_key], 1).astype(BF16)
        dvg = jnp.concatenate([d_value, d_gate], 1).astype(BF16)
        back = over(dqk, wqk) + over(dvg, wvg)
        dn[:, r] = back.astype(BF16).reshape(width, block, channels)
        new = (under(normed, dqk), under(normed, dvg), under(gated, row_cot))
        if gqk is None:
            gqk, gvg, gout = new
        else:
            gqk, gvg, gout = gqk + new[0], gvg + new[1], gout + new[2]
    part_rows = grads.shape[1]
    everything = jnp.concatenate([gqk, gvg, gout], 0).astype(BF16)
    for n in range(width):
        grads[n] = everything[n * part_rows : (n + 1) * part_rows]
    sources = ((grads, grads_in), (upd, upd_in), (dn, dn_in))
    for n, (src, dst) in enumerate(sources):
        exchange(src, dst, es.at[3 + n], er.at[3 + n])
    for src, dst in sources:
        dst[x] = src[x]

    sides = ((1, plus, acc_plus, send_plus, lp, ap), (-1, minus, acc_minus, send_minus, lm, am))
    for a in range(chain - 1, -1, -1):
        count = len(groups[a])
        for d in range(1, width):
            arrived(bias_in.at[0, pl.ds(0, count)], br.at[a, d])
        for delta in groups[a]:
            dest = place("row", -delta)
            pieces[dest] = add_up([bias_in[n, dest].astype(F32) for n in range(width)]).astype(BF16)
        if a == chain - 1:
            src = pieces.at[place("row", -half)]
            remote(src, acc_plus.at[a], ls, ap.at[a], "row", -HOP).start()
        for s, leaves, _, _, leaf_sem, _ in sides:
            for t in range(HOP - 1, 0, -1):
                src = pieces.at[place("row", -s * (t + HOP * a))]
                remote(src, leaves.at[a, t - 1], ls, leaf_sem.at[a], "row", -s * t).start()

    def relay(a):
        for s, leaves, acc, out, leaf_sem, acc_sem in sides:
            arrived(leaves.at[a], leaf_sem.at[a])
            value = pieces[place("row", -s * HOP * a)].astype(F32)
            value = value + add_up([leaves[a, t].astype(F32) for t in range(HOP - 1)])
            if s == 1 or a < chain - 1:
                arrived(acc.at[a], acc_sem.at[a])
                value = value + acc[a].astype(F32)
            out[a] = value.astype(BF16)
            remote(out.at[a], acc.at[a - 1], rs, acc_sem.at[a - 1], "row", -s * HOP).start()

    relay(chain - 1)
    exchanged(grads_in, es.at[3], er.at[3])
    summed = add_up([grads_in[n].astype(F32) for n in range(width)]).reshape(-1, HOP, channels)
    used = summed.shape[0]
    shares[pl.ds(0, used)] = summed.astype(BF16)
    shares[pl.ds(used, length - used)] = jnp.zeros((length - used, HOP, channels), BF16)
    to_all_rows(lambda step: shares.at[place("row", step)], shares_in.at[z], ss, lambda step: sr)
    for a in range(chain - 2, 0, -1):
        relay(a)
        if a == chain - 2:
            exchanged(upd_in, es.at[4], er.at[4])
            other = remote(upd_in, upd_other, cs.at[0], cr.at[0], "chan", 1)
            other.start()
            shares_in[z] = shares[z]
    other.wait()
    update[...] = (upd_in[...].astype(F32) + upd_other[...].astype(F32)).astype(BF16)
    exchanged(dn_in, es.at[5], er.at[5])
    tile = pieces[z].astype(F32)
    for s, leaves, acc, out, leaf_sem, acc_sem in sides:
        arrived(leaves.at[0], leaf_sem.at[0])
        arrived(acc.at[0], acc_sem.at[0])
        tile = tile + add_up([leaves[0, t].astype(F32) for t in range(HOP - 1)])
        tile = tile + acc[0].astype(F32)
    columns = jnp.transpose(tile)
    sums = [None, None]
    for j in range(full_rows):
        normed = normed_own[j * block : (j + 1) * block].astype(F32)
        added = dn_in[j // row_count, j % row_count].astype(F32)
        for h in range(2):
            column = columns[h * block : (h + 1) * block, j : j + 1]
            added = added + column * w_rows[h : h + 1, :]
            term = normed * column
            sums[h] = term if sums[h] is None else sums[h] + term
        dn_mine[j // row_count, j % row_count] = added.astype(BF16)
    sums = [jnp.sum(term, 0, keepdims=True) for term in sums]
    bias_own[...] = jnp.concatenate(sums, 0)
    for d in range(1, width):
        remote(bias_own, bias_x.at[x], ws, wr.at[d], "col", d).start()
    bias_x[x] = bias_own[...]
    other = remote(dn_mine, dn_other, cs.at[1], cr.at[1], "chan", 1)
    other.start()

    arrived(shares_in.at[pl.ds(0, length - 1)], sr)
    share_own[...] = jnp.sum(shares_in[...].astype(F32), 0).astype(BF16)
    to_all_rows(lambda step: share_own, share_all.at[x, z], fs, lambda step: fr.at[step % length])
    exchanged(bias_x, ws, wr)
    bias_row[...] = jnp.sum(bias_x[...], 0)
    to_all_rows(lambda step: bias_row, bias_all.at[z], vs, lambda step: vr)
    for d in range(1, width):
        remote(share_own, share_all.at[x, z], fxs, fxr.at[d], "col", d).start()
    share_all[x, z] = share_own[...]
    bias_all[z] = bias_row[...]

    other.wait()
    d_total = dn_mine[...].astype(F32) + dn_other[...].astype(F32)
    d_total = d_total.reshape(full_rows * block, channels)
    centred = d_total - jnp.mean(d_total, -1, keepdims=True)
    centred = centred - standard * jnp.mean(d_total * standard, -1, keepdims=True)
    grad[...] = (inverse * centred).astype(BF16).reshape(grad.shape)

    for step in by_distance(length):
        slot = share_all.at[x, place("row", -step)]
        arrived(slot, fr.at[step % length])
        for d in range(1, width):
            remote(slot, slot, fxs, fxr.at[d], "col", d).start()
    arrived(bias_all.at[pl.ds(0, length - 1)], vr)
    for d in range(1, width):
        arrived(share_all.at[place("col", -d)], fxr.at[d])
    for ref, sem in ((bias_all, vs), (share_all.at[0], fs), (shares, ss)):
        arrived(ref.at[pl.ds(0, length - 1)], sem)
    arrived(share_all.at[pl.ds(0, width - 1)], fxs)
    arrived(bias_in.at[pl.ds(0, width - 1)], bs)
    arrived(pieces.at[pl.ds(0, 2 * (HOP - 1) * chain + 1)], ls)
    arrived(pieces.at[pl.ds(0, 2 * (chain - 1))], rs)


def finish_kernel(tokens, update_in, grad_in, share_all, bias_all, update, grad, qkvg, bias, out):
    update[...] = update_in[...]
    grad[...] = grad_in[...]
    _, channels, cols = qkvg.shape
    total = 2 * channels + cols
    used = total // share_all.shape[0] // HOP
    rows = share_all[:, pl.ds(0, used)].astype(F32).reshape(total, channels) / tokens
    for p in range(2):
        part = rows[p * channels : (p + 1) * channels]
        qkvg[2 * p] = part[:, :cols]
        qkvg[2 * p + 1] = part[:, cols:]
    out[...] = rows[2 * channels :]
    both = jnp.sum(bias_all[...], 0) / tokens
    both = jnp.concatenate([both, jnp.zeros((6, channels), F32)], 0)
    bias[...] = jnp.transpose(both)[:, :2]


def call(kernel, name, identity, outs, scratch, *args):
    params = dict(vmem_limit_bytes=24 * 2**20)
    if identity is not None:
        params.update(collective_id=identity, has_side_effects=True)
    vmem = pl.BlockSpec(memory_space=pltpu.VMEM)
    return pl.pallas_call(
        kernel,
        out_shape=[jax.ShapeDtypeStruct(shape, kind) for shape, kind in outs],
        in_specs=[vmem] * len(args),
        out_specs=[vmem] * len(outs),
        scratch_shapes=scratch,
        compiler_params=pltpu.CompilerParams(**params),
        name=name,
    )(*args)


def on_device(pair_rep, pair_mask, w_qkvg, w_bias, w_out, cotangent):
    full_rows, block, channels = pair_rep.shape
    length, width = lax.axis_size("row"), lax.axis_size("col")
    cols = w_qkvg.shape[2]
    heads = w_bias.shape[1]
    scale = (cols // heads) ** (-0.5)
    tokens = width * block
    span = heads * block
    tiled = (width, full_rows // width, block, channels)
    part = (2 * channels + cols) // width
    chain = length // 2 // HOP
    message = (full_rows, span)
    V = pltpu.VMEM
    gathered = (width, length) + message
    share = (HOP, channels)
    tile = V(tiled, BF16)
    scratch = [V(message, F32), V(gathered, F32), tile, tile]
    scratch += [V(message, F32), V((width,) + message, F32)]
    scratch += [V(gathered, BF16)] * 2 + [tile] * 7
    scratch += [V((width, part, channels), BF16)] * 2 + [V((length,) + message, BF16)]
    scratch += [V((chain, HOP - 1) + message, BF16)] * 2 + [V((chain,) + message, BF16)] * 4
    scratch += [V((length,) + share, BF16)] * 2 + [V(share, BF16)]
    scratch += [V((heads, channels), F32), V((width, heads, channels), F32)]
    scratch += [V((heads, channels), F32)]
    scratch += [DMA, DMA((length,)), DMA, DMA((width,))]
    scratch += [DMA((6,)), DMA((6, width)), DMA, DMA((chain, width))]
    scratch += [DMA] + [DMA((chain,))] * 4 + [DMA, DMA((2,)), DMA((2,))]
    scratch += [DMA, DMA, DMA, DMA((length,)), DMA, DMA((width,))]
    scratch += [DMA, DMA((width,)), DMA, DMA]
    update, grad, share_all, bias_all = call(
        functools.partial(whole_kernel, scale),
        "whole",
        0,
        [
            (tiled, BF16),
            (tiled, BF16),
            ((width, length) + share, BF16),
            ((length, heads, channels), F32),
        ],
        scratch,
        pair_rep.reshape(tiled),
        cotangent.reshape(tiled),
        pair_mask,
        w_qkvg,
        w_bias,
        w_out,
    )
    shape = pair_rep.shape
    update, grad, qkvg, bias_grad, out = call(
        functools.partial(finish_kernel, tokens),
        "finish",
        None,
        [
            (tiled, BF16),
            (tiled, BF16),
            (w_qkvg.shape, F32),
            (w_bias.shape, F32),
            (w_out.shape, F32),
        ],
        [],
        update,
        grad,
        share_all,
        bias_all,
    )
    return (update.reshape(shape), grad.reshape(shape), qkvg, bias_grad, out)


def solution(mesh):
    in_specs = (
        P(("groups", "row"), "col", None),
        P(("groups", "row"), "col"),
        P(None, None, "chan"),
        P(None, "chan"),
        P("chan", None),
        P(("groups", "row"), "col", None),
    )
    out_specs = (
        P(("groups", "row"), "col", None),
        P(("groups", "row"), "col", None),
        P("groups", None, "chan"),
        P("groups", "chan"),
        P("chan", "groups"),
    )
    return jax.shard_map(
        on_device, mesh=mesh, in_specs=in_specs, out_specs=out_specs, check_vma=False
    )
```

time: 132 us -> 115 us (0.87)
  Pallas kernels: 123 us -> 110 us
  other arithmetic: 2.5 us -> 0 us
    pallas_call x3 -> x2, Pallas kernels: 123 us -> 110 us  [call(): pl.pallas_call(kernel, out_shape=[jax.ShapeDtypeStruct(shape, kind) for s...]
    reduce_sum x3 -> x0, other arithmetic: 1.51 us -> none  [the longest x1 1.11 us: on_device(): centred = values - jnp.mean(values, -1, keepdims=True)]
    unnamed x18 -> x12, local copies, waits for them, and re-layouts: 3.47 us -> 4.12 us
where the time goes in v2:
time: 115 us
  Pallas kernels  110 us (96%)
  local copies, waits for them, and re-layouts  4.12 us (4%)
    pallas_call x2, Pallas kernels, call(): pl.pallas_call(kernel, out_shape=[jax.ShapeDtypeStruct(shape, kind) for s...  110 us
    unnamed x12, local copies, waits for them, and re-layouts  4.12 us

profile of v2, /device:TPU:40, one launch (start us, length us, event | category | flops | bytes accessed | tf_op | source)
XLA Modules:
  0.0 115.1 jit_solution(5666703714120861297)
XLA Ops:
  0.6 0.0 copy-start
  0.6 0.8 copy.12.w_bias
  1.5 0.0 copy-start.2
  1.5 0.0 copy-start.3
  1.5 1.0 copy.11.w_qkvg
  2.5 0.0 copy-done
  2.5 0.0 copy-done.2
  2.5 0.0 copy-done.3
  2.5 0.0 copy-start.1
  2.5 0.9 copy-done.1
  3.4 109.5 %whole.1 = (bf16[4,2,64,128]{3,2,1,0:T(8,128)(2,1)S(1)}, bf16[4,2,64,128]{3,2,1,0:T(8,128)(2,1)S(1)}, bf16[4,32,4,128]{3,2,1,0:T(4,128)(2,1)S(1)}, f32[32,2,128]{2,1,0:T(2,128)S(1)}) custom-call(bf16[4,2,64,128]{3,2,1,0:T(8,128)(2,1)S(1)} %bitcast.4, bf16[4,2,64,128]{3,2,1,0:T(8,128)(2,1)S(1)} %bitcast.5, s32[8,64]{1,0:T(8,128)S(1)} %copy-done.3, ...), custom_call_target="tpu_custom_call" | custom-call | tf_op jit(solution)/shard_map/whole/pallas_call | solution.py:420
  112.9 0.8 finish.1
  113.6 0.6 copy.14
  114.3 0.8 copy.13
Async XLA Ops:
  0.6 1.8 %copy-start = (bf16[8,64,128]{2,1,0:T(8,128)(2,1)S(1)}, bf16[8,64,128]{2,1,0:T(8,128)(2,1)}, u32[]{:S(2)}) copy-start(bf16[8,64,128]{2,1,0:T(8,128)(2,1)} %param.6) | copy-start | bytes 393220
  1.5 1.0 copy-start.2
  1.5 1.0 copy-start.3
  2.5 0.9 copy-start.1

commit v3 on v2

--- a/solution.py
+++ b/solution.py
@@ -127,20 +127,18 @@
 
 
 def whole_kernel(
-    scale, pair, cot, mask, w_qkvg, w_bias, w_out, update, grad, share_all, bias_all,
-    piece, bias, rows, cots, mask_own, masks, d_bias, bias_in, upd, upd_in, upd_other,
-    dn, dn_in, dn_mine, dn_other, grads, grads_in, pieces, plus, minus, acc_plus, acc_minus,
-    send_plus, send_minus, shares, shares_in, share_own, bias_own, bias_x, bias_row,
-    gzs, gzr, gxs, gxr, es, er, bs, br, ls, lp, lm, ap, am, rs, cs, cr, ss, sr, fs, fr, fxs, fxr,
-    ws, wr, vs, vr,
+    scale, pair_far, cot_far, mask_far, w_qkvg_far, w_bias_far, w_out_far, update, grad, share_all,
+    bias_all, pair, cot, mask, w_qkvg, w_bias, w_out, piece, bias, rows, cots, mask_own, masks,
+    d_bias, bias_in, upd, upd_in, upd_other, dn, dn_in, dn_mine, dn_other, grads, grads_in, pieces,
+    tiles, shares, shares_in, share_own, bias_own, bias_x, bias_row, ins, gzs, gzr, gxs, gxr, es,
+    er, bs, br, ls, lr, cs, cr, ss, sr, fs, fr, fxs, fxr, ws, wr, vs, vr,
 ):
     length, width = lax.axis_size("row"), lax.axis_size("col")
     x, z = lax.axis_index("col"), lax.axis_index("row")
     _, row_count, block, channels = pair.shape
     cols = w_out.shape[0]
     size = cols // 2
-    tokens, span, half = width * block, 2 * block, length // 2
-    chain = half // HOP
+    tokens, span = width * block, 2 * block
     full_rows = width * row_count
     steps = [("chan", 1)] + [("col", d) for d in range(1, width)]
     steps += [("row", s * t) for t in range(1, HOP + 1) for s in (1, -1)]
@@ -150,21 +148,38 @@
             barrier, inc=1, device_id={axis: place(axis, step)}, device_id_type=MESH
         )
 
+    loads = [
+        pltpu.make_async_copy(src, dst, ins.at[n])
+        for n, (src, dst) in enumerate(
+            (
+                (pair_far, pair),
+                (w_bias_far, w_bias),
+                (mask_far, mask),
+                (w_qkvg_far, w_qkvg),
+                (cot_far, cot),
+                (w_out_far, w_out),
+            )
+        )
+    ]
+    for load in loads:
+        load.start()
+    for load in loads[:2]:
+        load.wait()
     standard, inverse = standardized(pair[...].reshape(full_rows * block, channels))
     normed_own = standard.astype(BF16)
-    line = lax.broadcasted_iota(jnp.int32, (channels, channels), 0)
-    eye = (line == lax.broadcasted_iota(jnp.int32, (channels, channels), 1)).astype(BF16)
-    w_rows = under(w_bias[...], eye)
-    flat = over(w_rows.astype(BF16), normed_own)
+    w_rows = w_bias[...].astype(F32)
+    flat = over(w_bias[...], normed_own)
     lines = []
     for j in range(full_rows):
         part = flat[:, j * block : (j + 1) * block]
         lines += [jnp.concatenate([part[0:1], part[1:2]], 1)]
     piece[...] = jnp.concatenate(lines, 0)
+    for load in loads[2:]:
+        load.wait()
     valid = MASK_BIG * (mask[...].astype(F32) - 1.0)
     mask_own[...] = jnp.concatenate([valid, valid], 1)
-    wqk = jnp.concatenate([w_qkvg[0], w_qkvg[1]], 1)
-    wvg = jnp.concatenate([w_qkvg[2], w_qkvg[3]], 1)
+    wqk = jnp.concatenate([w_qkvg[0], w_qkvg[1]], 0)
+    wvg = jnp.concatenate([w_qkvg[2], w_qkvg[3]], 0)
     pl.semaphore_wait(barrier, len(steps))
 
     head_lane = lax.broadcasted_iota(jnp.int32, (block, cols), 1) < size
@@ -205,7 +220,7 @@
         for r in range(row_count):
             normed = standardized(rows[:, r].reshape(tokens, channels))[0].astype(BF16)
             row_cot = cots[:, r].reshape(tokens, channels)
-            qk, vg = plain(normed, wqk), plain(normed, wvg)
+            qk, vg = over(normed, wqk), over(normed, wvg)
             query = (qk[:, :cols] * scale).astype(BF16)
             key2 = doubled(qk[:, cols:]).astype(BF16)
             value2 = doubled(vg[:, :cols]).astype(BF16)
@@ -249,18 +264,19 @@
         saved += [(weights_b, attended, d_scores_b)]
     for n in range(width):
         d_bias[n] = bias_sum[n].reshape(length, full_rows, span).astype(BF16)
-    groups = []
-    for a in range(chain):
-        group = [s * (HOP * a + t) for t in range(1, HOP) for s in (1, -1)]
-        group += [s * HOP * a for s in (1, -1)] if a else [0]
-        groups += [group + [half] if a == chain - 1 else group]
-    for a in range(chain - 1, -1, -1):
-        for delta in groups[a]:
-            dest = place("row", -delta)
-            for d in range(1, width):
-                remote(
-                    d_bias.at[place("col", d), dest], bias_in.at[x, dest], bs, br.at[a, d], "col", d
-                ).start()
+    order = list(reversed([0] + by_distance(length)))
+    quarter = length // 4
+    groups = [order[n * quarter : (n + 1) * quarter] for n in range(4)]
+
+    def send_group(n):
+        for delta in groups[n]:
+            dest = place("row", delta)
+            for d in (2, 1, 3):
+                src = d_bias.at[place("col", d), dest]
+                remote(src, bias_in.at[x, dest], bs, br.at[n, d], "col", d).start()
+
+    send_group(0)
+    send_group(1)
     bias_in[x] = d_bias[x]
 
     gqk = gvg = gout = None
@@ -275,9 +291,9 @@
         d_value = halved(under(weights_b, d_attended))
         dqk = jnp.concatenate([d_query, d_key], 1).astype(BF16)
         dvg = jnp.concatenate([d_value, d_gate], 1).astype(BF16)
-        back = over(dqk, wqk) + over(dvg, wvg)
+        back = plain(dqk, wqk) + plain(dvg, wvg)
         dn[:, r] = back.astype(BF16).reshape(width, block, channels)
-        new = (under(normed, dqk), under(normed, dvg), under(gated, row_cot))
+        new = (under(dqk, normed), under(dvg, normed), under(gated, row_cot))
         if gqk is None:
             gqk, gvg, gout = new
         else:
@@ -287,61 +303,45 @@
     for n in range(width):
         grads[n] = everything[n * part_rows : (n + 1) * part_rows]
     sources = ((grads, grads_in), (upd, upd_in), (dn, dn_in))
-    for n, (src, dst) in enumerate(sources):
-        exchange(src, dst, es.at[3 + n], er.at[3 + n])
+    exchange(grads, grads_in, es.at[3], er.at[3])
+    send_group(2)
+    send_group(3)
+    exchange(dn, dn_in, es.at[5], er.at[5])
+    exchange(upd, upd_in, es.at[4], er.at[4])
     for src, dst in sources:
         dst[x] = src[x]
 
-    sides = ((1, plus, acc_plus, send_plus, lp, ap), (-1, minus, acc_minus, send_minus, lm, am))
-    for a in range(chain - 1, -1, -1):
-        count = len(groups[a])
+    def send_tiles(n):
         for d in range(1, width):
-            arrived(bias_in.at[0, pl.ds(0, count)], br.at[a, d])
-        for delta in groups[a]:
-            dest = place("row", -delta)
-            pieces[dest] = add_up([bias_in[n, dest].astype(F32) for n in range(width)]).astype(BF16)
-        if a == chain - 1:
-            src = pieces.at[place("row", -half)]
-            remote(src, acc_plus.at[a], ls, ap.at[a], "row", -HOP).start()
-        for s, leaves, _, _, leaf_sem, _ in sides:
-            for t in range(HOP - 1, 0, -1):
-                src = pieces.at[place("row", -s * (t + HOP * a))]
-                remote(src, leaves.at[a, t - 1], ls, leaf_sem.at[a], "row", -s * t).start()
-
-    def relay(a):
-        for s, leaves, acc, out, leaf_sem, acc_sem in sides:
-            arrived(leaves.at[a], leaf_sem.at[a])
-            value = pieces[place("row", -s * HOP * a)].astype(F32)
-            value = value + add_up([leaves[a, t].astype(F32) for t in range(HOP - 1)])
-            if s == 1 or a < chain - 1:
-                arrived(acc.at[a], acc_sem.at[a])
-                value = value + acc[a].astype(F32)
-            out[a] = value.astype(BF16)
-            remote(out.at[a], acc.at[a - 1], rs, acc_sem.at[a - 1], "row", -s * HOP).start()
-
-    relay(chain - 1)
+            arrived(bias_in.at[0, pl.ds(0, quarter)], br.at[n, d])
+        for delta in groups[n]:
+            dest = place("row", delta)
+            pieces[dest] = add_up([bias_in[m, dest].astype(F32) for m in range(width)]).astype(BF16)
+        for delta in groups[n]:
+            if delta:
+                src = pieces.at[place("row", delta)]
+                remote(src, tiles.at[z], ls, lr, "row", delta).start()
+
+    send_tiles(0)
+    send_tiles(1)
     exchanged(grads_in, es.at[3], er.at[3])
     summed = add_up([grads_in[n].astype(F32) for n in range(width)]).reshape(-1, HOP, channels)
     used = summed.shape[0]
     shares[pl.ds(0, used)] = summed.astype(BF16)
     shares[pl.ds(used, length - used)] = jnp.zeros((length - used, HOP, channels), BF16)
     to_all_rows(lambda step: shares.at[place("row", step)], shares_in.at[z], ss, lambda step: sr)
-    for a in range(chain - 2, 0, -1):
-        relay(a)
-        if a == chain - 2:
-            exchanged(upd_in, es.at[4], er.at[4])
-            other = remote(upd_in, upd_other, cs.at[0], cr.at[0], "chan", 1)
-            other.start()
-            shares_in[z] = shares[z]
+    send_tiles(2)
+    send_tiles(3)
+    tiles[z] = pieces[z]
+    shares_in[z] = shares[z]
+    exchanged(dn_in, es.at[5], er.at[5])
+    exchanged(upd_in, es.at[4], er.at[4])
+    other = remote(upd_in, upd_other, cs.at[0], cr.at[0], "chan", 1)
+    other.start()
     other.wait()
     update[...] = (upd_in[...].astype(F32) + upd_other[...].astype(F32)).astype(BF16)
-    exchanged(dn_in, es.at[5], er.at[5])
-    tile = pieces[z].astype(F32)
-    for s, leaves, acc, out, leaf_sem, acc_sem in sides:
-        arrived(leaves.at[0], leaf_sem.at[0])
-        arrived(acc.at[0], acc_sem.at[0])
-        tile = tile + add_up([leaves[0, t].astype(F32) for t in range(HOP - 1)])
-        tile = tile + acc[0].astype(F32)
+    arrived(tiles.at[pl.ds(0, length - 1)], lr)
+    tile = jnp.sum(tiles[...].astype(F32), 0)
     columns = jnp.transpose(tile)
     sums = [None, None]
     for j in range(full_rows):
@@ -361,12 +361,12 @@
     other = remote(dn_mine, dn_other, cs.at[1], cr.at[1], "chan", 1)
     other.start()
 
+    exchanged(bias_x, ws, wr)
+    bias_row[...] = jnp.sum(bias_x[...], 0)
+    to_all_rows(lambda step: bias_row, bias_all.at[z], vs, lambda step: vr)
     arrived(shares_in.at[pl.ds(0, length - 1)], sr)
     share_own[...] = jnp.sum(shares_in[...].astype(F32), 0).astype(BF16)
     to_all_rows(lambda step: share_own, share_all.at[x, z], fs, lambda step: fr.at[step % length])
-    exchanged(bias_x, ws, wr)
-    bias_row[...] = jnp.sum(bias_x[...], 0)
-    to_all_rows(lambda step: bias_row, bias_all.at[z], vs, lambda step: vr)
     for d in range(1, width):
         remote(share_own, share_all.at[x, z], fxs, fxr.at[d], "col", d).start()
     share_all[x, z] = share_own[...]
@@ -391,36 +391,30 @@
         arrived(ref.at[pl.ds(0, length - 1)], sem)
     arrived(share_all.at[pl.ds(0, width - 1)], fxs)
     arrived(bias_in.at[pl.ds(0, width - 1)], bs)
-    arrived(pieces.at[pl.ds(0, 2 * (HOP - 1) * chain + 1)], ls)
-    arrived(pieces.at[pl.ds(0, 2 * (chain - 1))], rs)
+    arrived(pieces.at[pl.ds(0, length - 1)], ls)
 
 
 def finish_kernel(tokens, update_in, grad_in, share_all, bias_all, update, grad, qkvg, bias, out):
     update[...] = update_in[...]
     grad[...] = grad_in[...]
-    _, channels, cols = qkvg.shape
-    total = 2 * channels + cols
+    _, cols, channels = qkvg.shape
+    total = 4 * cols + out.shape[0]
     used = total // share_all.shape[0] // HOP
     rows = share_all[:, pl.ds(0, used)].astype(F32).reshape(total, channels) / tokens
-    for p in range(2):
-        part = rows[p * channels : (p + 1) * channels]
-        qkvg[2 * p] = part[:, :cols]
-        qkvg[2 * p + 1] = part[:, cols:]
-    out[...] = rows[2 * channels :]
-    both = jnp.sum(bias_all[...], 0) / tokens
-    both = jnp.concatenate([both, jnp.zeros((6, channels), F32)], 0)
-    bias[...] = jnp.transpose(both)[:, :2]
-
-
-def call(kernel, name, identity, outs, scratch, *args):
-    params = dict(vmem_limit_bytes=24 * 2**20)
+    qkvg[...] = rows[: 4 * cols].reshape(qkvg.shape)
+    out[...] = rows[4 * cols :]
+    bias[...] = jnp.sum(bias_all[...], 0) / tokens
+
+
+def call(kernel, name, identity, outs, scratch, *args, near=pltpu.VMEM):
+    params = dict(vmem_limit_bytes=60 * 2**20)
     if identity is not None:
         params.update(collective_id=identity, has_side_effects=True)
     vmem = pl.BlockSpec(memory_space=pltpu.VMEM)
     return pl.pallas_call(
         kernel,
         out_shape=[jax.ShapeDtypeStruct(shape, kind) for shape, kind in outs],
-        in_specs=[vmem] * len(args),
+        in_specs=[pl.BlockSpec(memory_space=near)] * len(args),
         out_specs=[vmem] * len(outs),
         scratch_shapes=scratch,
         compiler_params=pltpu.CompilerParams(**params),
@@ -438,23 +432,31 @@
     span = heads * block
     tiled = (width, full_rows // width, block, channels)
     part = (2 * channels + cols) // width
-    chain = length // 2 // HOP
     message = (full_rows, span)
     V = pltpu.VMEM
     gathered = (width, length) + message
     share = (HOP, channels)
     tile = V(tiled, BF16)
-    scratch = [V(message, F32), V(gathered, F32), tile, tile]
+    stored = jnp.transpose(w_qkvg, (0, 2, 1))
+    args = (
+        pair_rep.reshape(tiled),
+        cotangent.reshape(tiled),
+        pair_mask,
+        stored,
+        w_bias.T,
+        w_out,
+    )
+    scratch = [V(arg.shape, arg.dtype) for arg in args]
+    scratch += [V(message, F32), V(gathered, F32), tile, tile]
     scratch += [V(message, F32), V((width,) + message, F32)]
     scratch += [V(gathered, BF16)] * 2 + [tile] * 7
-    scratch += [V((width, part, channels), BF16)] * 2 + [V((length,) + message, BF16)]
-    scratch += [V((chain, HOP - 1) + message, BF16)] * 2 + [V((chain,) + message, BF16)] * 4
+    scratch += [V((width, part, channels), BF16)] * 2 + [V((length,) + message, BF16)] * 2
     scratch += [V((length,) + share, BF16)] * 2 + [V(share, BF16)]
     scratch += [V((heads, channels), F32), V((width, heads, channels), F32)]
     scratch += [V((heads, channels), F32)]
-    scratch += [DMA, DMA((length,)), DMA, DMA((width,))]
-    scratch += [DMA((6,)), DMA((6, width)), DMA, DMA((chain, width))]
-    scratch += [DMA] + [DMA((chain,))] * 4 + [DMA, DMA((2,)), DMA((2,))]
+    scratch += [DMA((len(args),)), DMA, DMA((length,)), DMA, DMA((width,))]
+    scratch += [DMA((6,)), DMA((6, width)), DMA, DMA((4, width))]
+    scratch += [DMA, DMA, DMA((2,)), DMA((2,))]
     scratch += [DMA, DMA, DMA, DMA((length,)), DMA, DMA((width,))]
     scratch += [DMA, DMA((width,)), DMA, DMA]
     update, grad, share_all, bias_all = call(
@@ -468,12 +470,8 @@
             ((length, heads, channels), F32),
         ],
         scratch,
-        pair_rep.reshape(tiled),
-        cotangent.reshape(tiled),
-        pair_mask,
-        w_qkvg,
-        w_bias,
-        w_out,
+        *args,
+        near=pltpu.HBM,
     )
     shape = pair_rep.shape
     update, grad, qkvg, bias_grad, out = call(
@@ -483,8 +481,8 @@
         [
             (tiled, BF16),
             (tiled, BF16),
-            (w_qkvg.shape, F32),
-            (w_bias.shape, F32),
+            (stored.shape, F32),
+            (w_bias.T.shape, F32),
             (w_out.shape, F32),
         ],
         [],
@@ -493,7 +491,8 @@
         share_all,
         bias_all,
     )
-    return (update.reshape(shape), grad.reshape(shape), qkvg, bias_grad, out)
+    qkvg = jnp.transpose(qkvg, (0, 2, 1))
+    return (update.reshape(shape), grad.reshape(shape), qkvg, bias_grad.T, out)
 
 
 def solution(mesh):

time: 115 us -> 110 us (0.957)
  local copies, waits for them, and re-layouts: 4.12 us -> 0 us
    unnamed x12 -> x0, local copies, waits for them, and re-layouts: 4.12 us -> none
where the time goes in v3:
time: 110 us
  Pallas kernels  109 us (99%)
    pallas_call x2, Pallas kernels, call(): pl.pallas_call(kernel, out_shape=[jax.ShapeDtypeStruct(shape, kind) for s...  109 us

profile of v3, /device:TPU:40, one launch (start us, length us, event | category | flops | bytes accessed | tf_op | source)
XLA Modules:
  0.0 109.9 jit_solution(7101558582236966781)
XLA Ops:
  0.6 107.5 %whole.1 = (bf16[4,2,64,128]{3,2,1,0:T(8,128)(2,1)}, bf16[4,2,64,128]{3,2,1,0:T(8,128)(2,1)}, bf16[4,32,4,128]{3,2,1,0:T(4,128)(2,1)}, f32[32,2,128]{2,1,0:T(2,128)}) custom-call(bf16[4,2,64,128]{3,2,1,0:T(8,128)(2,1)} %bitcast.8, bf16[4,2,64,128]{3,2,1,0:T(8,128)(2,1)} %bitcast.9, s32[8,64]{1,0:T(8,128)} %mask_far.1, bf16[4,64,128]{2,1,0:T(8,128)(2,1)} %bitcast.10, ...), custom_call_target="tpu_custom_call" | custom-call | tf_op jit(solution)/shard_map/whole/pallas_call | solution.py:414
  108.1 1.8 %finish.1 = (bf16[4,2,64,128]{3,2,1,0:T(8,128)(2,1)}, bf16[4,2,64,128]{3,2,1,0:T(8,128)(2,1)}, f32[4,64,128]{2,1,0:T(8,128)}, f32[2,128]{1,0:T(2,128)}, f32[64,128]{1,0:T(8,128)}) custom-call(bf16[4,2,64,128]{3,2,1,0:T(8,128)(2,1)} %get-tuple-element.14.update_in, bf16[4,2,64,128]{3,2,1,0:T(8,128)(2,1)} %get-tuple-element.15.grad_in, ...), custom_call_target="tpu_custom_call" | custom-call | tf_op jit(solution)/shard_map/finish/pallas_call | solution.py:414

commit v4 on v3

--- a/solution.py
+++ b/solution.py
@@ -36,58 +36,58 @@
     pltpu.make_async_copy(dst, dst, recv).wait()
 
 
-def gather_everywhere(piece, out, zs, zr, xs, xr, beside):
+def gather_everywhere(piece, out, zs, zr, xs, xr, gaps):
     length, width = lax.axis_size("row"), lax.axis_size("col")
     x, half = lax.axis_index("col"), length // 2
     last = half // HOP
 
-    def slot_of(delta):
-        return out.at[x, place("row", -delta)]
-
     def along_row(src, delta, steps):
         for step in steps:
-            recv = zr.at[(delta + step) % length]
-            remote(src, slot_of(delta), zs, recv, "row", step).start()
-
-    def along_col(src, delta):
-        for d in range(1, width):
-            remote(src, slot_of(delta), xs, xr.at[d], "col", d).start()
-
-    along_row(piece, 0, [s * t for t in (HOP, 3, 2, 1) for s in (1, -1)])
-    along_col(piece, 0)
-    out[x, lax.axis_index("row")] = piece[...]
-    result = beside()
-    for a in range(1, last + 1):
+            k = (delta + step) % length
+            remote(src, out.at[x, k], zs, zr.at[k], "row", step).start()
+
+    def along_col(src, first, count):
+        slots = out.at[x, pl.ds(first, count)]
+        for d in (2, 1, 3):
+            remote(slots if src is None else src, slots, xs, xr.at[d], "col", d).start()
+
+    def wait(delta):
+        arrived(out.at[x, delta % length], zr.at[delta % length])
+
+    along_row(piece.at[0], 0, [s * t for t in (HOP, 3, 2, 1) for s in (1, -1)])
+    along_col(piece, 0, 1)
+    out[x, 0] = piece[0]
+    gaps[0]()
+    for a in range(1, last):
         for s in (1, -1):
-            if a == last:
-                continue
-            delta = s * HOP * a
-            arrived(slot_of(delta), zr.at[delta % length])
+            wait(s * HOP * a)
             far = [s * HOP] if (s == 1 or a < last - 1) else []
-            along_row(slot_of(delta), delta, far + [s * t for t in (3, 2, 1)])
+            along_row(out.at[x, s * HOP * a % length], s * HOP * a, far + [s * t for t in (3, 2, 1)])
         for s in (1, -1):
-            if a < last:
-                along_col(slot_of(s * HOP * a), s * HOP * a)
             for t in range(1, HOP):
-                delta = s * (HOP * (a - 1) + t)
-                arrived(slot_of(delta), zr.at[delta % length])
-                along_col(slot_of(delta), delta)
-    arrived(slot_of(half), zr.at[half])
-    along_col(slot_of(half), half)
+                wait(s * (HOP * (a - 1) + t))
+            along_col(None, HOP * (a - 1) + 1 if s == 1 else length - HOP * a, HOP)
+        gaps[a]()
+    for t in range(1, HOP):
+        for s in (1, -1):
+            wait(s * (half - HOP + t))
+    along_col(None, half + 1, HOP - 1)
+    along_col(None, half - HOP + 1, HOP - 1)
+    wait(half)
+    along_col(None, half, 1)
     for d in range(1, width):
         arrived(out.at[place("col", -d)], xr.at[d])
     arrived(out.at[0, pl.ds(0, length - 1)], zs)
     arrived(out.at[pl.ds(0, width - 1)], xs)
-    return result
 
 
 def by_distance(length):
     return [s * t for t in range(1, length // 2) for s in (1, -1)] + [length // 2]
 
 
-def to_all_rows(src_of, dst, send, recv_of):
+def to_all_rows(src_of, dst_of, send, recv_of):
     for step in reversed(by_distance(lax.axis_size("row"))):
-        remote(src_of(step), dst, send, recv_of(step), "row", step).start()
+        remote(src_of(step), dst_of(step), send, recv_of(step), "row", step).start()
 
 
 def exchange(src, dst, xs, xr):
@@ -131,7 +131,7 @@
     bias_all, pair, cot, mask, w_qkvg, w_bias, w_out, piece, bias, rows, cots, mask_own, masks,
     d_bias, bias_in, upd, upd_in, upd_other, dn, dn_in, dn_mine, dn_other, grads, grads_in, pieces,
     tiles, shares, shares_in, share_own, bias_own, bias_x, bias_row, ins, gzs, gzr, gxs, gxr, es,
-    er, bs, br, ls, lr, cs, cr, ss, sr, fs, fr, fxs, fxr, ws, wr, vs, vr,
+    er, rs, rr, hs, hr, bs, br, ls, lr, cs, cr, ss, sr, fs, fr, fxs, fxr, ws, wr, vs, vr,
 ):
     length, width = lax.axis_size("row"), lax.axis_size("col")
     x, z = lax.axis_index("col"), lax.axis_index("row")
@@ -173,7 +173,7 @@
     for j in range(full_rows):
         part = flat[:, j * block : (j + 1) * block]
         lines += [jnp.concatenate([part[0:1], part[1:2]], 1)]
-    piece[...] = jnp.concatenate(lines, 0)
+    piece[0] = jnp.concatenate(lines, 0)
     for load in loads[2:]:
         load.wait()
     valid = MASK_BIG * (mask[...].astype(F32) - 1.0)
@@ -208,40 +208,67 @@
         second = reduced(jnp.where(lane, empty, both), axis=1, keepdims=True)
         return jnp.where(lane, first, second)
 
-    def projections():
-        exchange(pair, rows, es.at[0], er.at[0])
-        exchange(cot, cots, es.at[1], er.at[1])
-        for d in range(1, width):
+    core = lax.axis_index("chan")
+    halves = ((pair, rows), (cot, cots))
+    known = []
+
+    def start_exchange():
+        for n, (src, dst) in enumerate(halves):
+            for d in (2, 1, 3):
+                half = src.at[place("col", d), core]
+                remote(half, dst.at[x, core], rs.at[n, d], rr.at[n, d], "col", d).start()
+        for d in (2, 1, 3):
             remote(mask_own, masks.at[x], es.at[2], er.at[2, d], "col", d).start()
         rows[x], cots[x], masks[x] = pair[x], cot[x], mask_own[...]
-        for n, dst in enumerate((rows, cots, masks)):
-            exchanged(dst, es.at[n], er.at[n])
-        result = []
-        for r in range(row_count):
-            normed = standardized(rows[:, r].reshape(tokens, channels))[0].astype(BF16)
-            row_cot = cots[:, r].reshape(tokens, channels)
-            qk, vg = over(normed, wqk), over(normed, wvg)
-            query = (qk[:, :cols] * scale).astype(BF16)
-            key2 = doubled(qk[:, cols:]).astype(BF16)
-            value2 = doubled(vg[:, :cols]).astype(BF16)
-            gate = jax.nn.sigmoid(vg[:, cols:])
-            d_gated = over(row_cot, w_out[...])
-            d_attended = (d_gated * gate).astype(BF16)
-            scores = over(query, key2)
-            d_weights = over(d_attended, value2)
-            result += [
-                (normed, row_cot, query, key2, value2, gate, d_gated, d_attended, scores, d_weights)
-            ]
-        return result
-
-    known = gather_everywhere(piece, bias, gzs, gzr, gxs, gxr, projections)
+
+    def hand_over():
+        for n, (src, dst) in enumerate(halves):
+            for d in range(1, width):
+                half = dst.at[place("col", -d), core]
+                arrived(half, rr.at[n, d])
+                remote(half, half, hs.at[n, d], hr.at[n, d], "chan", 1).start()
+        for n, (src, dst) in enumerate(halves):
+            for d in range(1, width):
+                arrived(src.at[0, 0], rs.at[n, d])
+
+    def project(r):
+        normed = standardized(rows[:, r].reshape(tokens, channels))[0].astype(BF16)
+        row_cot = cots[:, r].reshape(tokens, channels)
+        qk, vg = over(normed, wqk), over(normed, wvg)
+        query = (qk[:, :cols] * scale).astype(BF16)
+        key2 = doubled(qk[:, cols:]).astype(BF16)
+        value2 = doubled(vg[:, :cols]).astype(BF16)
+        gate = jax.nn.sigmoid(vg[:, cols:])
+        d_gated = over(row_cot, w_out[...])
+        d_attended = (d_gated * gate).astype(BF16)
+        scores = over(query, key2)
+        d_weights = over(d_attended, value2)
+        known.append(
+            (normed, row_cot, query, key2, value2, gate, d_gated, d_attended, scores, d_weights)
+        )
+
+    def first_row():
+        for n, (_, dst) in enumerate(halves):
+            for d in range(1, width):
+                arrived(dst.at[place("col", -d), 1 - core], hr.at[n, d])
+                arrived(dst.at[0, 0], hs.at[n, d])
+        exchanged(masks, es.at[2], er.at[2])
+        project(0)
+
+    def other_rows():
+        for r in range(1, row_count):
+            project(r)
+
+    gaps = (start_exchange, hand_over, first_row, other_rows)
+    gather_everywhere(piece, bias, gzs, gzr, gxs, gxr, gaps)
+    blocks = [lax.rem(z + length - b, length) for b in range(length)]
 
     bias_sum = [None] * width
     saved = []
     for r in range(row_count):
         _, _, _, _, value2, _, _, d_attended, scores, d_weights = known[r]
         parts = [
-            (scores[:, n * span : (n + 1) * span] + bias[n].reshape(tokens, span))
+            (scores[:, n * span : (n + 1) * span] + jnp.concatenate([bias[n, k] for k in blocks], 0))
             + masks[n, pl.ds(x * row_count + r, 1), :]
             for n in range(width)
         ]
@@ -263,17 +290,20 @@
         d_scores_b = jnp.concatenate([d.astype(BF16) for d in d_scores], 1)
         saved += [(weights_b, attended, d_scores_b)]
     for n in range(width):
-        d_bias[n] = bias_sum[n].reshape(length, full_rows, span).astype(BF16)
-    order = list(reversed([0] + by_distance(length)))
-    quarter = length // 4
-    groups = [order[n * quarter : (n + 1) * quarter] for n in range(4)]
+        for b in range(length):
+            part = bias_sum[n][b * full_rows : (b + 1) * full_rows]
+            d_bias[n, lax.rem(b + length - z, length)] = part.astype(BF16)
+    quarter, half = length // 4, length // 2
+    step = quarter // 2
+    groups = [((half - step, quarter),)]
+    groups += [((half - n * step, step), (half + (n - 1) * step, step)) for n in range(2, 5)]
 
     def send_group(n):
-        for delta in groups[n]:
-            dest = place("row", delta)
+        for first, count in groups[n]:
+            slots = pl.ds(first, count)
             for d in (2, 1, 3):
-                src = d_bias.at[place("col", d), dest]
-                remote(src, bias_in.at[x, dest], bs, br.at[n, d], "col", d).start()
+                src = d_bias.at[place("col", d), slots]
+                remote(src, bias_in.at[x, slots], bs, br.at[n, d], "col", d).start()
 
     send_group(0)
     send_group(1)
@@ -314,13 +344,14 @@
     def send_tiles(n):
         for d in range(1, width):
             arrived(bias_in.at[0, pl.ds(0, quarter)], br.at[n, d])
-        for delta in groups[n]:
-            dest = place("row", delta)
-            pieces[dest] = add_up([bias_in[m, dest].astype(F32) for m in range(width)]).astype(BF16)
-        for delta in groups[n]:
-            if delta:
-                src = pieces.at[place("row", delta)]
-                remote(src, tiles.at[z], ls, lr, "row", delta).start()
+        slots = []
+        for first, count in groups[n]:
+            parts = [bias_in[m, first : first + count].astype(F32) for m in range(width)]
+            pieces[first : first + count] = add_up(parts).astype(BF16)
+            slots += range(first, first + count)
+        for k in sorted(slots, key=lambda k: -min(k, length - k)):
+            if k:
+                remote(pieces.at[k], tiles.at[k], ls, lr, "row", k).start()
 
     send_tiles(0)
     send_tiles(1)
@@ -329,11 +360,16 @@
     used = summed.shape[0]
     shares[pl.ds(0, used)] = summed.astype(BF16)
     shares[pl.ds(used, length - used)] = jnp.zeros((length - used, HOP, channels), BF16)
-    to_all_rows(lambda step: shares.at[place("row", step)], shares_in.at[z], ss, lambda step: sr)
+    to_all_rows(
+        lambda step: shares.at[place("row", step)],
+        lambda step: shares_in.at[step % length],
+        ss,
+        lambda step: sr,
+    )
     send_tiles(2)
     send_tiles(3)
-    tiles[z] = pieces[z]
-    shares_in[z] = shares[z]
+    tiles[0] = pieces[0]
+    shares_in[0] = shares[z]
     exchanged(dn_in, es.at[5], er.at[5])
     exchanged(upd_in, es.at[4], er.at[4])
     other = remote(upd_in, upd_other, cs.at[0], cr.at[0], "chan", 1)
@@ -346,31 +382,40 @@
     sums = [None, None]
     for j in range(full_rows):
         normed = normed_own[j * block : (j + 1) * block].astype(F32)
+        for h in range(2):
+            term = normed * columns[h * block : (h + 1) * block, j : j + 1]
+            sums[h] = term if sums[h] is None else sums[h] + term
+    sums = [jnp.sum(term, 0, keepdims=True) for term in sums]
+    bias_own[...] = jnp.concatenate(sums, 0)
+    for d in (2, 1, 3):
+        remote(bias_own, bias_x.at[x], ws, wr.at[d], "col", d).start()
+    bias_x[x] = bias_own[...]
+    for j in range(full_rows):
         added = dn_in[j // row_count, j % row_count].astype(F32)
         for h in range(2):
             column = columns[h * block : (h + 1) * block, j : j + 1]
             added = added + column * w_rows[h : h + 1, :]
-            term = normed * column
-            sums[h] = term if sums[h] is None else sums[h] + term
         dn_mine[j // row_count, j % row_count] = added.astype(BF16)
-    sums = [jnp.sum(term, 0, keepdims=True) for term in sums]
-    bias_own[...] = jnp.concatenate(sums, 0)
-    for d in range(1, width):
-        remote(bias_own, bias_x.at[x], ws, wr.at[d], "col", d).start()
-    bias_x[x] = bias_own[...]
     other = remote(dn_mine, dn_other, cs.at[1], cr.at[1], "chan", 1)
     other.start()
 
+    arrived(shares_in.at[pl.ds(0, length - 1)], sr)
+    share_own[...] = jnp.sum(shares_in[...].astype(F32), 0).astype(BF16)
+    to_all_rows(
+        lambda step: share_own,
+        lambda step: share_all.at[x, z],
+        fs,
+        lambda step: fr.at[step % length],
+    )
     exchanged(bias_x, ws, wr)
     bias_row[...] = jnp.sum(bias_x[...], 0)
-    to_all_rows(lambda step: bias_row, bias_all.at[z], vs, lambda step: vr)
-    arrived(shares_in.at[pl.ds(0, length - 1)], sr)
-    share_own[...] = jnp.sum(shares_in[...].astype(F32), 0).astype(BF16)
-    to_all_rows(lambda step: share_own, share_all.at[x, z], fs, lambda step: fr.at[step % length])
+    to_all_rows(
+        lambda step: bias_row, lambda step: bias_all.at[step % length], vs, lambda step: vr
+    )
     for d in range(1, width):
         remote(share_own, share_all.at[x, z], fxs, fxr.at[d], "col", d).start()
     share_all[x, z] = share_own[...]
-    bias_all[z] = bias_row[...]
+    bias_all[0] = bias_row[...]
 
     other.wait()
     d_total = dn_mine[...].astype(F32) + dn_other[...].astype(F32)
@@ -447,7 +492,7 @@
         w_out,
     )
     scratch = [V(arg.shape, arg.dtype) for arg in args]
-    scratch += [V(message, F32), V(gathered, F32), tile, tile]
+    scratch += [V((1,) + message, F32), V(gathered, F32), tile, tile]
     scratch += [V(message, F32), V((width,) + message, F32)]
     scratch += [V(gathered, BF16)] * 2 + [tile] * 7
     scratch += [V((width, part, channels), BF16)] * 2 + [V((length,) + message, BF16)] * 2
@@ -455,7 +500,7 @@
     scratch += [V((heads, channels), F32), V((width, heads, channels), F32)]
     scratch += [V((heads, channels), F32)]
     scratch += [DMA((len(args),)), DMA, DMA((length,)), DMA, DMA((width,))]
-    scratch += [DMA((6,)), DMA((6, width)), DMA, DMA((4, width))]
+    scratch += [DMA((6,)), DMA((6, width))] + [DMA((2, width))] * 4 + [DMA, DMA((4, width))]
     scratch += [DMA, DMA, DMA((2,)), DMA((2,))]
     scratch += [DMA, DMA, DMA, DMA((length,)), DMA, DMA((width,))]
     scratch += [DMA, DMA((width,)), DMA, DMA]

time: 110 us -> 106 us (0.964)
  Pallas kernels: 109 us -> 105 us
    pallas_call x2, Pallas kernels: 109 us -> 105 us  [call(): pl.pallas_call(kernel, out_shape=[jax.ShapeDtypeStruct(shape, kind) for s...]
where the time goes in v4:
time: 106 us
  Pallas kernels  105 us (99%)
    pallas_call x2, Pallas kernels, call(): pl.pallas_call(kernel, out_shape=[jax.ShapeDtypeStruct(shape, kind) for s...  105 us

profile of v4, /device:TPU:40, one launch (start us, length us, event | category | flops | bytes accessed | tf_op | source)
XLA Modules:
  0.0 105.7 jit_solution(11125405444674958673)
XLA Ops:
  0.6 103.3 %whole.1 = (bf16[4,2,64,128]{3,2,1,0:T(8,128)(2,1)}, bf16[4,2,64,128]{3,2,1,0:T(8,128)(2,1)}, bf16[4,32,4,128]{3,2,1,0:T(4,128)(2,1)}, f32[32,2,128]{2,1,0:T(2,128)}) custom-call(bf16[4,2,64,128]{3,2,1,0:T(8,128)(2,1)} %bitcast.8, bf16[4,2,64,128]{3,2,1,0:T(8,128)(2,1)} %bitcast.9, s32[8,64]{1,0:T(8,128)} %mask_far.1, bf16[4,64,128]{2,1,0:T(8,128)(2,1)} %bitcast.10, ...), custom_call_target="tpu_custom_call" | custom-call | tf_op jit(solution)/shard_map/whole/pallas_call | solution.py:459
  103.9 1.8 %finish.1 = (bf16[4,2,64,128]{3,2,1,0:T(8,128)(2,1)}, bf16[4,2,64,128]{3,2,1,0:T(8,128)(2,1)}, f32[4,64,128]{2,1,0:T(8,128)}, f32[2,128]{1,0:T(2,128)}, f32[64,128]{1,0:T(8,128)}) custom-call(bf16[4,2,64,128]{3,2,1,0:T(8,128)(2,1)} %get-tuple-element.14.update_in, bf16[4,2,64,128]{3,2,1,0:T(8,128)(2,1)} %get-tuple-element.15.grad_in, ...), custom_call_target="tpu_custom_call" | custom-call | tf_op jit(solution)/shard_map/finish/pallas_call | solution.py:459

commit v5 on v4

--- a/solution.py
+++ b/solution.py
@@ -306,7 +306,6 @@
                 remote(src, bias_in.at[x, slots], bs, br.at[n, d], "col", d).start()
 
     send_group(0)
-    send_group(1)
     bias_in[x] = d_bias[x]
 
     gqk = gvg = gout = None
@@ -334,8 +333,8 @@
         grads[n] = everything[n * part_rows : (n + 1) * part_rows]
     sources = ((grads, grads_in), (upd, upd_in), (dn, dn_in))
     exchange(grads, grads_in, es.at[3], er.at[3])
-    send_group(2)
-    send_group(3)
+    for n in range(1, 4):
+        send_group(n)
     exchange(dn, dn_in, es.at[5], er.at[5])
     exchange(upd, upd_in, es.at[4], er.at[4])
     for src, dst in sources:
@@ -354,22 +353,21 @@
                 remote(pieces.at[k], tiles.at[k], ls, lr, "row", k).start()
 
     send_tiles(0)
-    send_tiles(1)
     exchanged(grads_in, es.at[3], er.at[3])
     summed = add_up([grads_in[n].astype(F32) for n in range(width)]).reshape(-1, HOP, channels)
-    used = summed.shape[0]
-    shares[pl.ds(0, used)] = summed.astype(BF16)
-    shares[pl.ds(used, length - used)] = jnp.zeros((length - used, HOP, channels), BF16)
-    to_all_rows(
-        lambda step: shares.at[place("row", step)],
-        lambda step: shares_in.at[step % length],
-        ss,
-        lambda step: sr,
-    )
-    send_tiles(2)
-    send_tiles(3)
+    shares[...] = summed.astype(BF16)
+    used = shares.shape[0]
+    for step in reversed(by_distance(length)):
+        dest = place("row", step)
+
+        @pl.when(dest < used)
+        def _():
+            src = shares.at[dest]
+            remote(src, shares_in.at[step % length], ss, sr, "row", step).start()
+
+    for n in range(1, 4):
+        send_tiles(n)
     tiles[0] = pieces[0]
-    shares_in[0] = shares[z]
     exchanged(dn_in, es.at[5], er.at[5])
     exchanged(upd_in, es.at[4], er.at[4])
     other = remote(upd_in, upd_other, cs.at[0], cr.at[0], "chan", 1)
@@ -399,22 +397,23 @@
     other = remote(dn_mine, dn_other, cs.at[1], cr.at[1], "chan", 1)
     other.start()
 
-    arrived(shares_in.at[pl.ds(0, length - 1)], sr)
-    share_own[...] = jnp.sum(shares_in[...].astype(F32), 0).astype(BF16)
-    to_all_rows(
-        lambda step: share_own,
-        lambda step: share_all.at[x, z],
-        fs,
-        lambda step: fr.at[step % length],
-    )
+    @pl.when(z < used)
+    def _():
+        shares_in[0] = shares[z]
+        arrived(shares_in.at[pl.ds(0, length - 1)], sr)
+        share_own[...] = jnp.sum(shares_in[...].astype(F32), 0).astype(BF16)
+        slot = share_all.at[x, z]
+        for step in reversed(by_distance(length)):
+            remote(share_own, slot, fs, fr.at[step % length], "row", step).start()
+        for d in (2, 1, 3):
+            remote(share_own, slot, fxs, fxr.at[d], "col", d).start()
+        share_all[x, z] = share_own[...]
+
     exchanged(bias_x, ws, wr)
     bias_row[...] = jnp.sum(bias_x[...], 0)
     to_all_rows(
         lambda step: bias_row, lambda step: bias_all.at[step % length], vs, lambda step: vr
     )
-    for d in range(1, width):
-        remote(share_own, share_all.at[x, z], fxs, fxr.at[d], "col", d).start()
-    share_all[x, z] = share_own[...]
     bias_all[0] = bias_row[...]
 
     other.wait()
@@ -425,15 +424,29 @@
     grad[...] = (inverse * centred).astype(BF16).reshape(grad.shape)
 
     for step in by_distance(length):
-        slot = share_all.at[x, place("row", -step)]
-        arrived(slot, fr.at[step % length])
-        for d in range(1, width):
-            remote(slot, slot, fxs, fxr.at[d], "col", d).start()
+        source = place("row", -step)
+
+        @pl.when(source < used)
+        def _():
+            slot = share_all.at[x, source]
+            arrived(slot, fr.at[step % length])
+            for d in (2, 1, 3):
+                remote(slot, slot, fxs, fxr.at[d], "col", d).start()
+
     arrived(bias_all.at[pl.ds(0, length - 1)], vr)
     for d in range(1, width):
         arrived(share_all.at[place("col", -d)], fxr.at[d])
-    for ref, sem in ((bias_all, vs), (share_all.at[0], fs), (shares, ss)):
-        arrived(ref.at[pl.ds(0, length - 1)], sem)
+    arrived(bias_all.at[pl.ds(0, length - 1)], vs)
+
+    @pl.when(z < used)
+    def _():
+        arrived(shares_in.at[pl.ds(0, length - 1)], fs)
+        arrived(shares.at[pl.ds(0, used - 1)], ss)
+
+    @pl.when(z >= used)
+    def _():
+        arrived(shares, ss)
+
     arrived(share_all.at[pl.ds(0, width - 1)], fxs)
     arrived(bias_in.at[pl.ds(0, width - 1)], bs)
     arrived(pieces.at[pl.ds(0, length - 1)], ls)
@@ -444,15 +457,14 @@
     grad[...] = grad_in[...]
     _, cols, channels = qkvg.shape
     total = 4 * cols + out.shape[0]
-    used = total // share_all.shape[0] // HOP
-    rows = share_all[:, pl.ds(0, used)].astype(F32).reshape(total, channels) / tokens
+    rows = share_all[...].astype(F32).reshape(total, channels) / tokens
     qkvg[...] = rows[: 4 * cols].reshape(qkvg.shape)
     out[...] = rows[4 * cols :]
     bias[...] = jnp.sum(bias_all[...], 0) / tokens
 
 
 def call(kernel, name, identity, outs, scratch, *args, near=pltpu.VMEM):
-    params = dict(vmem_limit_bytes=60 * 2**20)
+    params = dict(vmem_limit_bytes=24 * 2**20)
     if identity is not None:
         params.update(collective_id=identity, has_side_effects=True)
     vmem = pl.BlockSpec(memory_space=pltpu.VMEM)
@@ -496,7 +508,7 @@
     scratch += [V(message, F32), V((width,) + message, F32)]
     scratch += [V(gathered, BF16)] * 2 + [tile] * 7
     scratch += [V((width, part, channels), BF16)] * 2 + [V((length,) + message, BF16)] * 2
-    scratch += [V((length,) + share, BF16)] * 2 + [V(share, BF16)]
+    scratch += [V((part // HOP,) + share, BF16), V((length,) + share, BF16), V(share, BF16)]
     scratch += [V((heads, channels), F32), V((width, heads, channels), F32)]
     scratch += [V((heads, channels), F32)]
     scratch += [DMA((len(args),)), DMA, DMA((length,)), DMA, DMA((width,))]
@@ -511,11 +523,11 @@
         [
             (tiled, BF16),
             (tiled, BF16),
-            ((width, length) + share, BF16),
+            ((width, part // HOP) + share, BF16),
             ((length, heads, channels), F32),
         ],
         scratch,
-        *args,
+        *(pltpu.with_memory_space_constraint(arg, pltpu.HBM) for arg in args),
         near=pltpu.HBM,
     )
     shape = pair_rep.shape

time: 106 us -> 104 us (0.981)
  Pallas kernels: 105 us -> 103 us
    pallas_call x2, Pallas kernels: 105 us -> 103 us  [call(): pl.pallas_call(kernel, out_shape=[jax.ShapeDtypeStruct(shape, kind) for s...]
where the time goes in v5:
time: 104 us
  Pallas kernels  103 us (99%)
    pallas_call x2, Pallas kernels, call(): pl.pallas_call(kernel, out_shape=[jax.ShapeDtypeStruct(shape, kind) for s...  103 us

profile of v5, /device:TPU:40, one launch (start us, length us, event | category | flops | bytes accessed | tf_op | source)
XLA Modules:
  0.0 103.9 jit_solution(16689568760870377463)
XLA Ops:
  0.6 102.5 %whole.1 = (bf16[4,2,64,128]{3,2,1,0:T(8,128)(2,1)S(1)}, bf16[4,2,64,128]{3,2,1,0:T(8,128)(2,1)S(1)}, bf16[4,20,4,128]{3,2,1,0:T(4,128)(2,1)S(1)}, f32[32,2,128]{2,1,0:T(2,128)S(1)}) custom-call(bf16[4,2,64,128]{3,2,1,0:T(8,128)(2,1)} %bitcast.8, bf16[4,2,64,128]{3,2,1,0:T(8,128)(2,1)} %bitcast.9, s32[8,64]{1,0:T(8,128)} %mask_far.1, ...), custom_call_target="tpu_custom_call" | custom-call | tf_op jit(solution)/shard_map/whole/pallas_call | solution.py:471
  103.1 0.8 finish.1

commit v6 on v5

--- a/solution.py
+++ b/solution.py
@@ -131,7 +131,7 @@
     bias_all, pair, cot, mask, w_qkvg, w_bias, w_out, piece, bias, rows, cots, mask_own, masks,
     d_bias, bias_in, upd, upd_in, upd_other, dn, dn_in, dn_mine, dn_other, grads, grads_in, pieces,
     tiles, shares, shares_in, share_own, bias_own, bias_x, bias_row, ins, gzs, gzr, gxs, gxr, es,
-    er, rs, rr, hs, hr, bs, br, ls, lr, cs, cr, ss, sr, fs, fr, fxs, fxr, ws, wr, vs, vr,
+    er, entered, bs, br, ls, lr, cs, cr, ss, sr, fs, fr, fxs, fxr, ws, wr, vs, vr,
 ):
     length, width = lax.axis_size("row"), lax.axis_size("col")
     x, z = lax.axis_index("col"), lax.axis_index("row")
@@ -140,12 +140,20 @@
     size = cols // 2
     tokens, span = width * block, 2 * block
     full_rows = width * row_count
-    steps = [("chan", 1)] + [("col", d) for d in range(1, width)]
+    steps = [("col", d) for d in range(1, width)]
     steps += [("row", s * t) for t in range(1, HOP + 1) for s in (1, -1)]
     barrier = pltpu.get_barrier_semaphore()
     for axis, step in steps:
         pl.semaphore_signal(
             barrier, inc=1, device_id={axis: place(axis, step)}, device_id_type=MESH
+        )
+
+    core = lax.axis_index("chan")
+
+    @pl.when(core == 0)
+    def _():
+        pl.semaphore_signal(
+            barrier, inc=1, device_id={"chan": place("chan", 1)}, device_id_type=MESH
         )
 
     loads = [
@@ -180,7 +188,14 @@
     mask_own[...] = jnp.concatenate([valid, valid], 1)
     wqk = jnp.concatenate([w_qkvg[0], w_qkvg[1]], 0)
     wvg = jnp.concatenate([w_qkvg[2], w_qkvg[3]], 0)
-    pl.semaphore_wait(barrier, len(steps))
+    pl.semaphore_wait(barrier, len(steps) + core)
+
+    @pl.when(core == 1)
+    def _():
+        pl.semaphore_signal(
+            entered, inc=1, device_id={"chan": place("chan", 1)}, device_id_type=MESH
+        )
+
 
     head_lane = lax.broadcasted_iota(jnp.int32, (block, cols), 1) < size
     lane = lax.broadcasted_iota(jnp.int32, (tokens, span), 1) < block
@@ -208,28 +223,14 @@
         second = reduced(jnp.where(lane, empty, both), axis=1, keepdims=True)
         return jnp.where(lane, first, second)
 
-    core = lax.axis_index("chan")
-    halves = ((pair, rows), (cot, cots))
     known = []
 
     def start_exchange():
-        for n, (src, dst) in enumerate(halves):
-            for d in (2, 1, 3):
-                half = src.at[place("col", d), core]
-                remote(half, dst.at[x, core], rs.at[n, d], rr.at[n, d], "col", d).start()
-        for d in (2, 1, 3):
+        exchange(pair, rows, es.at[0], er.at[0])
+        exchange(cot, cots, es.at[1], er.at[1])
+        for d in range(1, width):
             remote(mask_own, masks.at[x], es.at[2], er.at[2, d], "col", d).start()
         rows[x], cots[x], masks[x] = pair[x], cot[x], mask_own[...]
-
-    def hand_over():
-        for n, (src, dst) in enumerate(halves):
-            for d in range(1, width):
-                half = dst.at[place("col", -d), core]
-                arrived(half, rr.at[n, d])
-                remote(half, half, hs.at[n, d], hr.at[n, d], "chan", 1).start()
-        for n, (src, dst) in enumerate(halves):
-            for d in range(1, width):
-                arrived(src.at[0, 0], rs.at[n, d])
 
     def project(r):
         normed = standardized(rows[:, r].reshape(tokens, channels))[0].astype(BF16)
@@ -248,18 +249,15 @@
         )
 
     def first_row():
-        for n, (_, dst) in enumerate(halves):
-            for d in range(1, width):
-                arrived(dst.at[place("col", -d), 1 - core], hr.at[n, d])
-                arrived(dst.at[0, 0], hs.at[n, d])
-        exchanged(masks, es.at[2], er.at[2])
+        for n, dst in enumerate((rows, cots, masks)):
+            exchanged(dst, es.at[n], er.at[n])
         project(0)
 
     def other_rows():
         for r in range(1, row_count):
             project(r)
 
-    gaps = (start_exchange, hand_over, first_row, other_rows)
+    gaps = (start_exchange, lambda: None, first_row, other_rows)
     gather_everywhere(piece, bias, gzs, gzr, gxs, gxr, gaps)
     blocks = [lax.rem(z + length - b, length) for b in range(length)]
 
@@ -370,6 +368,11 @@
     tiles[0] = pieces[0]
     exchanged(dn_in, es.at[5], er.at[5])
     exchanged(upd_in, es.at[4], er.at[4])
+
+    @pl.when(core == 0)
+    def _():
+        pl.semaphore_wait(entered, 1)
+
     other = remote(upd_in, upd_other, cs.at[0], cr.at[0], "chan", 1)
     other.start()
     other.wait()
@@ -512,7 +515,7 @@
     scratch += [V((heads, channels), F32), V((width, heads, channels), F32)]
     scratch += [V((heads, channels), F32)]
     scratch += [DMA((len(args),)), DMA, DMA((length,)), DMA, DMA((width,))]
-    scratch += [DMA((6,)), DMA((6, width))] + [DMA((2, width))] * 4 + [DMA, DMA((4, width))]
+    scratch += [DMA((6,)), DMA((6, width)), pltpu.SemaphoreType.REGULAR, DMA, DMA((4, width))]
     scratch += [DMA, DMA, DMA((2,)), DMA((2,))]
     scratch += [DMA, DMA, DMA, DMA((length,)), DMA, DMA((width,))]
     scratch += [DMA, DMA((width,)), DMA, DMA]

time: 104 us -> 104 us (level)
  no operation moved by 1% of the time
where the time goes in v6:
time: 104 us
  Pallas kernels  103 us (99%)
    pallas_call x2, Pallas kernels, call(): pl.pallas_call(kernel, out_shape=[jax.ShapeDtypeStruct(shape, kind) for s...  103 us

profile of v6, /device:TPU:40, one launch (start us, length us, event | category | flops | bytes accessed | tf_op | source)
XLA Modules:
  0.0 103.6 jit_solution(6620333587882267593)
XLA Ops:
  0.6 102.2 %whole.1 = (bf16[4,2,64,128]{3,2,1,0:T(8,128)(2,1)S(1)}, bf16[4,2,64,128]{3,2,1,0:T(8,128)(2,1)S(1)}, bf16[4,20,4,128]{3,2,1,0:T(4,128)(2,1)S(1)}, f32[32,2,128]{2,1,0:T(2,128)S(1)}) custom-call(bf16[4,2,64,128]{3,2,1,0:T(8,128)(2,1)} %bitcast.8, bf16[4,2,64,128]{3,2,1,0:T(8,128)(2,1)} %bitcast.9, s32[8,64]{1,0:T(8,128)} %mask_far.1, ...), custom_call_target="tpu_custom_call" | custom-call | tf_op jit(solution)/shard_map/whole/pallas_call | solution.py:474
  102.8 0.8 finish.1

commit v7 on v5

--- a/solution.py
+++ b/solution.py
@@ -36,10 +36,11 @@
     pltpu.make_async_copy(dst, dst, recv).wait()
 
 
-def gather_everywhere(piece, out, zs, zr, xs, xr, gaps):
+def gather_everywhere(piece, out, zs, zr, xs, xr, hs, hr, gaps):
     length, width = lax.axis_size("row"), lax.axis_size("col")
     x, half = lax.axis_index("col"), length // 2
     last = half // HOP
+    core = lax.axis_index("chan")
 
     def along_row(src, delta, steps):
         for step in steps:
@@ -54,31 +55,59 @@
     def wait(delta):
         arrived(out.at[x, delta % length], zr.at[delta % length])
 
-    along_row(piece.at[0], 0, [s * t for t in (HOP, 3, 2, 1) for s in (1, -1)])
-    along_col(piece, 0, 1)
-    out[x, 0] = piece[0]
+    @pl.when(core == 0)
+    def _():
+        remote(piece.at[0, 0], piece.at[0, 0], hs.at[0], hr.at[0], "chan", 1).start()
+
+    @pl.when(core == 1)
+    def _():
+        arrived(piece.at[0, 0], hr.at[0])
+        along_row(piece.at[0], 0, [s * t for t in (HOP, 3, 2, 1) for s in (1, -1)])
+        along_col(piece, 0, 1)
+        out[x, 0] = piece[0]
+
     gaps[0]()
     for a in range(1, last):
-        for s in (1, -1):
-            wait(s * HOP * a)
-            far = [s * HOP] if (s == 1 or a < last - 1) else []
-            along_row(out.at[x, s * HOP * a % length], s * HOP * a, far + [s * t for t in (3, 2, 1)])
-        for s in (1, -1):
-            for t in range(1, HOP):
-                wait(s * (HOP * (a - 1) + t))
-            along_col(None, HOP * (a - 1) + 1 if s == 1 else length - HOP * a, HOP)
+
+        @pl.when(core == 1)
+        def _():
+            for s in (1, -1):
+                delta = s * HOP * a
+                wait(delta)
+                far = [s * HOP] if (s == 1 or a < last - 1) else []
+                along_row(out.at[x, delta % length], delta, far + [s * t for t in (3, 2, 1)])
+            for s in (1, -1):
+                for t in range(1, HOP):
+                    wait(s * (HOP * (a - 1) + t))
+                along_col(None, HOP * (a - 1) + 1 if s == 1 else length - HOP * a, HOP)
+
         gaps[a]()
-    for t in range(1, HOP):
-        for s in (1, -1):
-            wait(s * (half - HOP + t))
-    along_col(None, half + 1, HOP - 1)
-    along_col(None, half - HOP + 1, HOP - 1)
-    wait(half)
-    along_col(None, half, 1)
-    for d in range(1, width):
-        arrived(out.at[place("col", -d)], xr.at[d])
-    arrived(out.at[0, pl.ds(0, length - 1)], zs)
-    arrived(out.at[pl.ds(0, width - 1)], xs)
+
+    @pl.when(core == 1)
+    def _():
+        for t in range(1, HOP):
+            for s in (1, -1):
+                wait(s * (half - HOP + t))
+        along_col(None, half + 1, HOP - 1)
+        along_col(None, half - HOP + 1, HOP - 1)
+        wait(half)
+        along_col(None, half, 1)
+        for d in range(width):
+            column = place("col", -d)
+            if d:
+                arrived(out.at[column], xr.at[d])
+            slab = out.at[column, pl.ds(0, length), 0]
+            remote(slab, slab, hs.at[1 + d], hr.at[1 + d], "chan", 1).start()
+        arrived(out.at[0, pl.ds(0, length - 1)], zs)
+        arrived(out.at[pl.ds(0, width - 1)], xs)
+        for d in range(width):
+            arrived(out.at[0, pl.ds(0, half)], hs.at[1 + d])
+
+    @pl.when(core == 0)
+    def _():
+        for d in range(width):
+            arrived(out.at[0, pl.ds(0, half)], hr.at[1 + d])
+        arrived(piece.at[0, 0], hs.at[0])
 
 
 def by_distance(length):
@@ -131,7 +160,7 @@
     bias_all, pair, cot, mask, w_qkvg, w_bias, w_out, piece, bias, rows, cots, mask_own, masks,
     d_bias, bias_in, upd, upd_in, upd_other, dn, dn_in, dn_mine, dn_other, grads, grads_in, pieces,
     tiles, shares, shares_in, share_own, bias_own, bias_x, bias_row, ins, gzs, gzr, gxs, gxr, es,
-    er, rs, rr, hs, hr, bs, br, ls, lr, cs, cr, ss, sr, fs, fr, fxs, fxr, ws, wr, vs, vr,
+    er, rs, rr, hs, hr, gs, gr, bs, br, ls, lr, cs, cr, ss, sr, fs, fr, fxs, fxr, ws, wr, vs, vr,
 ):
     length, width = lax.axis_size("row"), lax.axis_size("col")
     x, z = lax.axis_index("col"), lax.axis_index("row")
@@ -173,7 +202,7 @@
     for j in range(full_rows):
         part = flat[:, j * block : (j + 1) * block]
         lines += [jnp.concatenate([part[0:1], part[1:2]], 1)]
-    piece[0] = jnp.concatenate(lines, 0)
+    piece[0, lax.axis_index("chan")] = jnp.concatenate(lines, 0)
     for load in loads[2:]:
         load.wait()
     valid = MASK_BIG * (mask[...].astype(F32) - 1.0)
@@ -260,7 +289,7 @@
             project(r)
 
     gaps = (start_exchange, hand_over, first_row, other_rows)
-    gather_everywhere(piece, bias, gzs, gzr, gxs, gxr, gaps)
+    gather_everywhere(piece, bias, gzs, gzr, gxs, gxr, gs, gr, gaps)
     blocks = [lax.rem(z + length - b, length) for b in range(length)]
 
     bias_sum = [None] * width
@@ -268,7 +297,7 @@
     for r in range(row_count):
         _, _, _, _, value2, _, _, d_attended, scores, d_weights = known[r]
         parts = [
-            (scores[:, n * span : (n + 1) * span] + jnp.concatenate([bias[n, k] for k in blocks], 0))
+            (scores[:, n * span : (n + 1) * span] + jnp.concatenate([bias[n, k, core] for k in blocks], 0))
             + masks[n, pl.ds(x * row_count + r, 1), :]
             for n in range(width)
         ]
@@ -504,7 +533,8 @@
         w_out,
     )
     scratch = [V(arg.shape, arg.dtype) for arg in args]
-    scratch += [V((1,) + message, F32), V(gathered, F32), tile, tile]
+    both = (lax.axis_size("chan"),) + message
+    scratch += [V((1,) + both, F32), V((width, length) + both, F32), tile, tile]
     scratch += [V(message, F32), V((width,) + message, F32)]
     scratch += [V(gathered, BF16)] * 2 + [tile] * 7
     scratch += [V((width, part, channels), BF16)] * 2 + [V((length,) + message, BF16)] * 2
@@ -512,7 +542,8 @@
     scratch += [V((heads, channels), F32), V((width, heads, channels), F32)]
     scratch += [V((heads, channels), F32)]
     scratch += [DMA((len(args),)), DMA, DMA((length,)), DMA, DMA((width,))]
-    scratch += [DMA((6,)), DMA((6, width))] + [DMA((2, width))] * 4 + [DMA, DMA((4, width))]
+    scratch += [DMA((6,)), DMA((6, width))] + [DMA((2, width))] * 4
+    scratch += [DMA((1 + width,)), DMA((1 + width,)), DMA, DMA((4, width))]
     scratch += [DMA, DMA, DMA((2,)), DMA((2,))]
     scratch += [DMA, DMA, DMA, DMA((length,)), DMA, DMA((width,))]
     scratch += [DMA, DMA((width,)), DMA, DMA]

time: 104 us -> 105 us (level)
  no operation moved by 1% of the time
where the time goes in v7:
time: 105 us; the launch traced here: 104 us
  Pallas kernels  104 us (99%)
    pallas_call x2, Pallas kernels, call(): pl.pallas_call(kernel, out_shape=[jax.ShapeDtypeStruct(shape, kind) for s...  104 us

profile of v7, /device:TPU:40, one launch (start us, length us, event | category | flops | bytes accessed | tf_op | source)
XLA Modules:
  0.0 104.5 jit_solution(9033511333009831593)
XLA Ops:
  0.6 103.0 %whole.1 = (bf16[4,2,64,128]{3,2,1,0:T(8,128)(2,1)S(1)}, bf16[4,2,64,128]{3,2,1,0:T(8,128)(2,1)S(1)}, bf16[4,20,4,128]{3,2,1,0:T(4,128)(2,1)S(1)}, f32[32,2,128]{2,1,0:T(2,128)S(1)}) custom-call(bf16[4,2,64,128]{3,2,1,0:T(8,128)(2,1)} %bitcast.8, bf16[4,2,64,128]{3,2,1,0:T(8,128)(2,1)} %bitcast.9, s32[8,64]{1,0:T(8,128)} %mask_far.1, ...), custom_call_target="tpu_custom_call" | custom-call | tf_op jit(solution)/shard_map/whole/pallas_call | solution.py:500
  103.7 0.8 finish.1

commit v8 on v5

--- a/solution.py
+++ b/solution.py
@@ -77,8 +77,6 @@
     along_col(None, half, 1)
     for d in range(1, width):
         arrived(out.at[place("col", -d)], xr.at[d])
-    arrived(out.at[0, pl.ds(0, length - 1)], zs)
-    arrived(out.at[pl.ds(0, width - 1)], xs)
 
 
 def by_distance(length):
@@ -91,7 +89,7 @@
 
 
 def exchange(src, dst, xs, xr):
-    for d in range(1, lax.axis_size("col")):
+    for d in (2, 1, 3):
         remote(
             src.at[place("col", d)], dst.at[lax.axis_index("col")], xs, xr.at[d], "col", d
         ).start()
@@ -227,10 +225,6 @@
                 half = dst.at[place("col", -d), core]
                 arrived(half, rr.at[n, d])
                 remote(half, half, hs.at[n, d], hr.at[n, d], "chan", 1).start()
-        for n, (src, dst) in enumerate(halves):
-            for d in range(1, width):
-                arrived(src.at[0, 0], rs.at[n, d])
-
     def project(r):
         normed = standardized(rows[:, r].reshape(tokens, channels))[0].astype(BF16)
         row_cot = cots[:, r].reshape(tokens, channels)
@@ -247,19 +241,15 @@
             (normed, row_cot, query, key2, value2, gate, d_gated, d_attended, scores, d_weights)
         )
 
-    def first_row():
+    def project_all():
         for n, (_, dst) in enumerate(halves):
             for d in range(1, width):
                 arrived(dst.at[place("col", -d), 1 - core], hr.at[n, d])
-                arrived(dst.at[0, 0], hs.at[n, d])
         exchanged(masks, es.at[2], er.at[2])
-        project(0)
-
-    def other_rows():
-        for r in range(1, row_count):
+        for r in range(row_count):
             project(r)
 
-    gaps = (start_exchange, hand_over, first_row, other_rows)
+    gaps = (start_exchange, lambda: None, hand_over, project_all)
     gather_everywhere(piece, bias, gzs, gzr, gxs, gxr, gaps)
     blocks = [lax.rem(z + length - b, length) for b in range(length)]
 
@@ -448,8 +438,14 @@
         arrived(shares, ss)
 
     arrived(share_all.at[pl.ds(0, width - 1)], fxs)
+    arrived(bias.at[0, pl.ds(0, length - 1)], gzs)
+    arrived(bias.at[pl.ds(0, width - 1)], gxs)
     arrived(bias_in.at[pl.ds(0, width - 1)], bs)
     arrived(pieces.at[pl.ds(0, length - 1)], ls)
+    for n, (src, dst) in enumerate(halves):
+        for d in range(1, width):
+            arrived(src.at[0, 0], rs.at[n, d])
+            arrived(dst.at[0, 0], hs.at[n, d])
 
 
 def finish_kernel(tokens, update_in, grad_in, share_all, bias_all, update, grad, qkvg, bias, out):

time: 104 us -> 104 us (level)
  no operation moved by 1% of the time
where the time goes in v8:
time: 104 us
  Pallas kernels  103 us (99%)
    pallas_call x2, Pallas kernels, call(): pl.pallas_call(kernel, out_shape=[jax.ShapeDtypeStruct(shape, kind) for s...  103 us

profile of v8, /device:TPU:40, one launch (start us, length us, event | category | flops | bytes accessed | tf_op | source)
XLA Modules:
  0.0 103.7 jit_solution(4117753344320027593)
XLA Ops:
  0.6 102.3 %whole.1 = (bf16[4,2,64,128]{3,2,1,0:T(8,128)(2,1)S(1)}, bf16[4,2,64,128]{3,2,1,0:T(8,128)(2,1)S(1)}, bf16[4,20,4,128]{3,2,1,0:T(4,128)(2,1)S(1)}, f32[32,2,128]{2,1,0:T(2,128)S(1)}) custom-call(bf16[4,2,64,128]{3,2,1,0:T(8,128)(2,1)} %bitcast.8, bf16[4,2,64,128]{3,2,1,0:T(8,128)(2,1)} %bitcast.9, s32[8,64]{1,0:T(8,128)} %mask_far.1, ...), custom_call_target="tpu_custom_call" | custom-call | tf_op jit(solution)/shard_map/whole/pallas_call | solution.py:467
  103.0 0.8 finish.1
